TPU v7x, 256 devices: a whole 4x4x8 slice. The times are simulated.
256 devices in a mesh: mol: 16 (over x_lo, y, core), grid: 16 (over x_hi, z).
Axes of the slice: x: 4 (x_hi: 2, x_lo: 2; x = x_hi * 2 + x_lo), y: 4, z: 8, core: 2. Of those that a mesh axis runs over, the one named last changes fastest.
Arguments:
- cells_start: int32 [131072], P('mol'), may hold values from 0 to 2097151
- moves: int32 [2, 3, 131072], P(None, None, 'mol'), may hold values from -1 to 1
- accepted: int32 [2, 131072], P(None, 'mol'), may hold values from 0 to 1
- bead_types: int32 [131072], P('mol'), may hold values from 0 to 1
Outputs:
- energy_change: float32 [2, 131072], P(None, 'mol')
- final_field: bfloat16 [64, 64, 1024], P('mol', 'grid')
All inputs are finite; a program needn't handle non-finite values.
Results may differ from a plain program's by a relative error of at most 0.0048.
Values may be sent and summed in bfloat16 or wider, within the bound.
No kernel may reach another device: no remote copies, remote signals or barrier semaphores. Data moves between devices by JAX's collectives and lax.ppermute only.
A program may use at most 64 MiB of HBM per device.

v0:
```python
import jax
import jax.numpy as jnp
from jax import lax
from jax.sharding import PartitionSpec as P

NX = 512
NY = 64
ZDEV = 4
STEPS = 2
SPREAD = 2


chi_mix = 1.0
kappa_comp = 0.5


def split_up(x, dim, size):
    shape = x.shape
    blocks = x.reshape(*shape[:dim], size, shape[dim] // size, *shape[dim + 1 :])
    return jnp.moveaxis(blocks, dim, 0)


def sum_at_owner(x, axis, dim):
    blocks = split_up(x, dim, lax.axis_size(axis))
    arrived = lax.all_to_all(blocks, axis, split_axis=0, concat_axis=0, tiled=True)
    return arrived.sum(axis=0)


def laid_out(blocks, dim):
    blocks = jnp.moveaxis(blocks, 0, dim)
    shape = blocks.shape
    return blocks.reshape(*shape[:dim], shape[dim] * shape[dim + 1], *shape[dim + 2 :])


def sent_to_all(x, axis):
    copies = jnp.broadcast_to(x, (lax.axis_size(axis), *x.shape))
    return lax.all_to_all(copies, axis, split_axis=0, concat_axis=0, tiled=True)


def collect(x, axis, dim):
    return laid_out(sent_to_all(x, axis), dim)


def of_everyone(x, axis):
    return sent_to_all(x, axis).astype(jnp.float32).sum(axis=0)


def kernel_rows(col_x):
    column = jnp.arange(NX, dtype=jnp.float32)
    distance = jnp.abs(column[None, :] - col_x.astype(jnp.float32)[:, None])
    distance = jnp.minimum(distance, NX - distance)
    weights = jnp.exp(-distance * distance / (2.0 * SPREAD * SPREAD))
    first = jnp.abs(column)
    first = jnp.minimum(first, NX - first)
    total = jnp.sum(jnp.exp(-first * first / (2.0 * SPREAD * SPREAD)))
    return (weights / total).astype(jnp.bfloat16)


def split_cell(cells):
    col_x = cells % NX
    row_y = cells // NX % NY
    plane_z = cells // (NX * NY)
    return (col_x, row_y, plane_z)


def move_cells(cells, shift, planes):
    col_x, row_y, plane_z = split_cell(cells)
    col_x = (col_x + shift[0]) % NX
    row_y = (row_y + shift[1]) % NY
    plane_z = (plane_z + shift[2]) % planes
    return (plane_z * NY + row_y) * NX + col_x


def deposit(positions, bead_types, slab, start, count):
    col_x, row_y, plane_z = split_cell(positions)
    inside = (plane_z // ZDEV == slab) & (row_y >= start) & (row_y < start + count)
    row_id = jnp.where(inside, row_y * ZDEV + plane_z - slab * ZDEV, -1)
    bead_count = positions.shape[0]
    block_size = min(1024, bead_count)
    row_total = count * ZDEV
    targets = lax.broadcasted_iota(jnp.int32, (row_total, block_size), 0)

    def add_block(block_id, total):
        begin = block_id * block_size
        rows_here = lax.dynamic_slice_in_dim(row_id, begin, block_size)
        cols_here = lax.dynamic_slice_in_dim(col_x, begin, block_size)
        types_here = lax.dynamic_slice_in_dim(bead_types, begin, block_size)
        onehot = (rows_here[None, :] == targets).astype(jnp.bfloat16)
        spread_rows = kernel_rows(cols_here)
        zeros_bf = jnp.zeros_like(spread_rows)
        first = jnp.where(types_here[:, None] == 0, spread_rows, zeros_bf)
        second = jnp.where(types_here[:, None] == 1, spread_rows, zeros_bf)
        columns = jnp.concatenate([first, second], axis=1)
        return total + jnp.dot(onehot, columns, preferred_element_type=jnp.float32)

    empty = jnp.zeros((row_total, 2 * NX), jnp.float32)
    total = lax.fori_loop(0, bead_count // block_size, add_block, empty)
    return total.reshape(count, ZDEV, 2 * NX)


def make_field(density):
    phi_a = density[:, :, :NX]
    phi_b = density[:, :, NX:]
    excess = kappa_comp * (phi_a + phi_b - 1.0)
    field_a = chi_mix * phi_b + excess
    field_b = chi_mix * phi_a + excess
    return jnp.concatenate([field_a, field_b], axis=2).astype(jnp.bfloat16)


def make_reader(points, bead_types, z_first, z_span):
    col_x, row_y, plane_z = split_cell(points)
    local_z = plane_z - z_first
    kinds = jnp.broadcast_to(bead_types[None, :], points.shape)
    column_id = kinds * NX + col_x

    def read_beads(carry, piece, start):
        span_rows = piece.shape[0]
        flat_table = piece.reshape(-1)
        valid = (row_y >= 0) & (row_y < span_rows) & (local_z >= 0) & (local_z < z_span)
        flat_index = jnp.where(valid, (row_y * z_span + local_z) * (2 * NX) + column_id, 0)
        picked = jnp.take(flat_table, flat_index).astype(jnp.float32)
        return jnp.where(valid, picked, 0.0)

    return read_beads


def local(cells_start, moves, accepted, bead_types):
    grid_count = lax.axis_size("grid")
    mol_count = lax.axis_size("mol")
    slab = lax.axis_index("grid")
    planes = ZDEV * grid_count
    bead_count = cells_start.shape[0]
    scale = NX * NY * planes / (bead_count * mol_count)
    band_rows = NY // mol_count
    positions = [cells_start]
    proposals = []
    for step in range(STEPS):
        proposed = move_cells(positions[step], moves[step], planes)
        proposals.append(proposed)
        positions.append(jnp.where(accepted[step] == 1, proposed, positions[step]))
    fields = []
    for step in range(STEPS):

        def step_term(start, count, current=positions[step]):
            return deposit(current, bead_types, slab, start, count)

        summed = sum_at_owner(step_term(jnp.int32(0), band_rows * lax.axis_size("mol")), "mol", 0)
        fields.append(make_field(scale * summed))
    changes = []
    for step in range(STEPS):
        points = jnp.stack([positions[step], proposals[step]])
        start_values = jnp.zeros(points.shape, jnp.float32)
        reader = make_reader(points, bead_types, slab * ZDEV, ZDEV)
        partial_values = reader(start_values, collect(fields[step], "mol", 0), jnp.int32(0))
        values = of_everyone(partial_values.astype(jnp.bfloat16), "grid").astype(jnp.float32)
        changes.append(values[1] - values[0])
    return (jnp.stack(changes), fields[STEPS - 1])


def solution(mesh):
    return jax.shard_map(
        local,
        mesh=mesh,
        in_specs=(P("mol"), P(None, None, "mol"), P(None, "mol"), P("mol")),
        out_specs=(P(None, "mol"), P("mol", "grid", None)),
        check_vma=False,
    )
```

profile of v0, /device:TPU:32, one launch (start us, length us, event | category | flops | bytes accessed | tf_op | source)
XLA Modules:
  0.0 375.2 jit_solution(1999360355959154496)
XLA Ops:
  3.8 32.8 %while.28 = (s32[]{:T(128)}, f32[256,1024]{1,0:T(8,128)S(1)}, s32[8192]{0:T(1024)S(1)}, s32[8192]{0:T(1024)}, s32[8192]{0:T(1024)S(1)}, /*index=5*/s32[]{:T(128)}, s32[]{:T(128)}, s32[]{:T(128)}, s32[]{:T(128)}) while((s32[]{:T(128)}, f32[256,1024]{1,0:T(8,128)S(1)}, s32[8192]{0:T(1024)S(1)}, s32[8192]{0:T(1024)}, ...), condition=%wide.region_2.3_spmd.clone, body=%wide.region_0.2_spmd.clone.sunk | while | flops 547624960 | bytes 6324393 | solution.py:97
  5.1 1.9 fusion.88
  9.2 1.9 fusion.88
  13.3 1.9 fusion.88
  37.9 5.6 %all-to-all-start = ((f32[16,4,4,1024]{3,2,1,0:T(4,128)}), f32[16,4,4,1024]{3,2,1,0:T(4,128)S(1)}, u32[]{:S(2)}, u32[]{:S(2)}) async-start(f32[16,4,4,1024]{3,2,1,0:T(4,128)} %reshape_reshape.12), calls=%async_computation | async-start | bytes 2097152 | tf_op jit(solution)/shard_map/all_to_all | solution.py:25
  43.6 42.7 %while.29 = (s32[]{:T(128)}, f32[256,1024]{1,0:T(8,128)}, s32[8192]{0:T(1024)S(1)}, s32[8192]{0:T(1024)S(1)}, s32[8192]{0:T(1024)S(1)}, /*index=5*/s32[]{:T(128)}, s32[]{:T(128)}, s32[]{:T(128)}, s32[]{:T(128)}) while((s32[]{:T(128)}, f32[256,1024]{1,0:T(8,128)}, s32[8192]{0:T(1024)S(1)}, s32[8192]{0:T(1024)S(1)}, ...), condition=%wide.region_7.9_spmd.clone, body=%wide.region_5.8_spmd.clone.sunk | while | flops 547624960 | bytes 6324393 | solution.py:97
  50.5 3.0 fusion.93
  55.9 3.0 fusion.93
  61.4 3.0 fusion.93
  66.9 3.0 fusion.93
  72.4 3.0 fusion.93
  77.9 3.0 fusion.93
  83.3 3.0 fusion.93
  87.5 2.6 reshape_reshape.14
  90.1 5.7 %all-to-all-start.3 = ((f32[16,4,4,1024]{3,2,1,0:T(4,128)}), f32[16,4,4,1024]{3,2,1,0:T(4,128)S(1)}, u32[]{:S(2)}, u32[]{:S(2)}) async-start(f32[16,4,4,1024]{3,2,1,0:T(4,128)} %reshape_reshape.14), calls=%async_computation.3 | async-start | bytes 2097152 | tf_op jit(solution)/shard_map/all_to_all | solution.py:25
  96.1 16.2 %all-to-all-done.3 = f32[16,4,4,1024]{3,2,1,0:T(4,128)S(1)} async-done(((f32[16,4,4,1024]{3,2,1,0:T(4,128)}), f32[16,4,4,1024]{3,2,1,0:T(4,128)S(1)}, u32[]{:S(2)}, u32[]{:S(2)}) %all-to-all-start.3) | async-done | bytes 1048608 | tf_op jit(solution)/shard_map/all_to_all | solution.py:25
  113.4 3.6 all-to-all-start.1
  117.3 10.5 %all-to-all-done.1 = bf16[16,4,4,1024]{3,2,1,0:T(4,128)(2,1)S(1)} async-done(((bf16[16,4,4,1024]{3,2,1,0:T(4,128)(2,1)}), bf16[16,4,4,1024]{3,2,1,0:T(4,128)(2,1)S(1)}, u32[]{:S(2)}, u32[]{:S(2)}) %all-to-all-start.1) | async-done | bytes 524320 | tf_op jit(solution)/shard_map/all_to_all | solution.py:37
  128.7 3.6 all-to-all-start.4
  132.4 100.9 %gather_fusion = bf16[16384]{0:T(1024)(128)(2,1)S(1)} fusion(bf16[262144]{0:T(1024)(128)(2,1)S(1)} %bitcast.18, s32[16384]{0:T(1024)S(1)} %broadcast_clamp_fusion.1), kind=kCustom, calls=%fused_computation.clone | custom fusion | bytes 131072 | tf_op jit(solution)/shard_map/jit(_take)/gather | solution.py:121
  234.9 10.8 %all-to-all-start.2 = ((bf16[16,2,8192]{2,1,0:T(2,128)(2,1)}), bf16[16,2,8192]{2,1,0:T(2,128)(2,1)S(1)}, u32[]{:S(2)}, u32[]{:S(2)}) async-start(bf16[16,2,8192]{2,1,0:T(2,128)(2,1)} %broadcast_in_dim.123), calls=%async_computation.2 | async-start | bytes 1048576 | tf_op jit(solution)/shard_map/all_to_all | solution.py:37
  245.7 100.9 %gather_fusion.1 = bf16[16384]{0:T(1024)(128)(2,1)S(1)} fusion(bf16[262144]{0:T(1024)(128)(2,1)S(1)} %bitcast.19, s32[16384]{0:T(1024)S(1)} %broadcast_clamp_fusion), kind=kCustom, calls=%fused_computation.1.clone | custom fusion | bytes 131072 | tf_op jit(solution)/shard_map/jit(_take)/gather | solution.py:121
  348.2 9.6 %all-to-all-start.5 = ((bf16[16,2,8192]{2,1,0:T(2,128)(2,1)}), bf16[16,2,8192]{2,1,0:T(2,128)(2,1)S(1)}, u32[]{:S(2)}, u32[]{:S(2)}) async-start(bf16[16,2,8192]{2,1,0:T(2,128)(2,1)} %broadcast_in_dim.125), calls=%async_computation.5 | async-start | bytes 1048576 | tf_op jit(solution)/shard_map/all_to_all | solution.py:37
  358.4 15.7 %all-to-all-done.5 = bf16[16,2,8192]{2,1,0:T(2,128)(2,1)S(1)} async-done(((bf16[16,2,8192]{2,1,0:T(2,128)(2,1)}), bf16[16,2,8192]{2,1,0:T(2,128)(2,1)S(1)}, u32[]{:S(2)}, u32[]{:S(2)}) %all-to-all-start.5) | async-done | bytes 524320 | tf_op jit(solution)/shard_map/all_to_all | solution.py:37
  (131 shorter events, 61.8 us)
Async XLA Ops:
  37.9 5.6 %copy-start.1 = (s32[8192]{0:T(1024)S(1)}, s32[8192]{0:T(1024)}, u32[]{:S(2)}) copy-start(s32[8192]{0:T(1024)} %get-tuple-element.452) | copy-start | bytes 98308
  37.9 52.2 %all-to-all-start = ((f32[16,4,4,1024]{3,2,1,0:T(4,128)}), f32[16,4,4,1024]{3,2,1,0:T(4,128)S(1)}, u32[]{:S(2)}, u32[]{:S(2)}) async-start(f32[16,4,4,1024]{3,2,1,0:T(4,128)} %reshape_reshape.12), calls=%async_computation | async-start | bytes 2097152 | tf_op jit(solution)/shard_map/all_to_all | solution.py:25
  43.6 42.7 %copy-start = (s32[8192]{0:T(1024)S(1)}, s32[8192]{0:T(1024)}, u32[]{:S(2)}) copy-start(s32[8192]{0:T(1024)} %param.10) | copy-start | bytes 98308
  90.1 22.3 %all-to-all-start.3 = ((f32[16,4,4,1024]{3,2,1,0:T(4,128)}), f32[16,4,4,1024]{3,2,1,0:T(4,128)S(1)}, u32[]{:S(2)}, u32[]{:S(2)}) async-start(f32[16,4,4,1024]{3,2,1,0:T(4,128)} %reshape_reshape.14), calls=%async_computation.3 | async-start | bytes 2097152 | tf_op jit(solution)/shard_map/all_to_all | solution.py:25
  113.4 14.4 %all-to-all-start.1 = ((bf16[16,4,4,1024]{3,2,1,0:T(4,128)(2,1)}), bf16[16,4,4,1024]{3,2,1,0:T(4,128)(2,1)S(1)}, u32[]{:S(2)}, u32[]{:S(2)}) async-start(bf16[16,4,4,1024]{3,2,1,0:T(4,128)(2,1)} %broadcast_in_dim.120), calls=%async_computation.1 | async-start | bytes 1048576 | tf_op jit(solution)/shard_map/all_to_all | solution.py:37
  117.2 15.2 %copy-start.2 = (bf16[4,4,1024]{2,1,0:T(4,128)(2,1)}, bf16[4,4,1024]{2,1,0:T(4,128)(2,1)S(1)}, u32[]{:S(2)}) copy-start(bf16[4,4,1024]{2,1,0:T(4,128)(2,1)S(1)} %pad_maximum_fusion.2) | copy-start | bytes 98308
  128.7 104.9 %all-to-all-start.4 = ((bf16[16,4,4,1024]{3,2,1,0:T(4,128)(2,1)}), bf16[16,4,4,1024]{3,2,1,0:T(4,128)(2,1)S(1)}, u32[]{:S(2)}, u32[]{:S(2)}) async-start(bf16[16,4,4,1024]{3,2,1,0:T(4,128)(2,1)} %broadcast_in_dim.124), calls=%async_computation.4 | async-start | bytes 1048576 | tf_op jit(solution)/shard_map/all_to_all | solution.py:37
  234.9 112.1 %all-to-all-start.2 = ((bf16[16,2,8192]{2,1,0:T(2,128)(2,1)}), bf16[16,2,8192]{2,1,0:T(2,128)(2,1)S(1)}, u32[]{:S(2)}, u32[]{:S(2)}) async-start(bf16[16,2,8192]{2,1,0:T(2,128)(2,1)} %broadcast_in_dim.123), calls=%async_computation.2 | async-start | bytes 1048576 | tf_op jit(solution)/shard_map/all_to_all | solution.py:37
  348.2 25.8 %all-to-all-start.5 = ((bf16[16,2,8192]{2,1,0:T(2,128)(2,1)}), bf16[16,2,8192]{2,1,0:T(2,128)(2,1)S(1)}, u32[]{:S(2)}, u32[]{:S(2)}) async-start(bf16[16,2,8192]{2,1,0:T(2,128)(2,1)} %broadcast_in_dim.125), calls=%async_computation.5 | async-start | bytes 1048576 | tf_op jit(solution)/shard_map/all_to_all | solution.py:37
where the time goes:
time: 378 us; the launch traced here: 375 us
  local copies, waits for them, and re-layouts  212 us (56%)
  other arithmetic  51.5 us (14%)
  waiting for transfers between devices  42.4 us (11%)
  starting transfers between devices  38.9 us (10%)
  matrix products  29.3 us (8%)
    gather x4, local copies, waits for them, and re-layouts, read_beads(): picked = jnp.take(flat_table, flat_index).astype(jnp.float32)  202 us
    select_n x16, other arithmetic, add_block(): first = jnp.where(types_here[:, None] == 0, spread_rows, zeros_bf)  29.8 us
    dot_general x16, matrix products, add_block(): return total + jnp.dot(onehot, columns, preferred_element_type=jnp.float32)  29.3 us
    all_to_all x4, starting transfers between devices, sent_to_all(): return lax.all_to_all(copies, axis, split_axis=0, concat_axis=0, tiled=True)  27.5 us
    all_to_all x4, waiting for transfers between devices, sent_to_all(): return lax.all_to_all(copies, axis, split_axis=0, concat_axis=0, tiled=True)  26.2 us
    all_to_all x2, waiting for transfers between devices, sum_at_owner(): lax.all_to_all(blocks, axis, split_axis=0, concat_axis=0, tiled=True)  16.2 us
    all_to_all x2, starting transfers between devices, sum_at_owner(): lax.all_to_all(blocks, axis, split_axis=0, concat_axis=0, tiled=True)  11.4 us
    reduce_sum x16, other arithmetic, kernel_rows(): total = jnp.sum(jnp.exp(-first * first / (2.0 * SPREAD * SPREAD)))  9.9 us
  transfers between devices with their start and end apart: 6, of which 3 were waited for; matrix products, arithmetic and copies ran while one was open for 67% of the time, Pallas kernels for 0%

commit v1 on v0

--- a/solution.py
+++ b/solution.py
@@ -1,6 +1,10 @@
+import functools
+
 import jax
 import jax.numpy as jnp
 from jax import lax
+from jax.experimental import pallas as pl
+from jax.experimental.pallas import tpu as pltpu
 from jax.sharding import PartitionSpec as P
 
 NX = 512
@@ -8,6 +12,15 @@
 ZDEV = 4
 STEPS = 2
 SPREAD = 2
+GROUPS = 16
+SLOTS = 128
+CHUNK = 256
+SETS = 4
+MSG = 80
+F32 = jnp.float32
+BF16 = jnp.bfloat16
+CONTRACT_LANES = (((1,), (1,)), ((), ()))
+CONTRACT_SUBLANES = (((0,), (0,)), ((), ()))
 
 
 chi_mix = 1.0
@@ -124,7 +137,7 @@
     return read_beads
 
 
-def local(cells_start, moves, accepted, bead_types):
+def any_spread(cells_start, moves, accepted, bead_types):
     grid_count = lax.axis_size("grid")
     mol_count = lax.axis_size("mol")
     slab = lax.axis_index("grid")
@@ -157,6 +170,233 @@
     return (jnp.stack(changes), fields[STEPS - 1])
 
 
+def one_hot(row, count, base=0):
+    width = row.shape[1]
+    tile = jnp.broadcast_to(row, (16, width)).astype(BF16)
+    iota = lax.broadcasted_iota(jnp.int32, (16, width), 0).astype(F32)
+    one = jnp.ones((16, width), BF16)
+    zero = jnp.zeros((16, width), BF16)
+    parts = [
+        jnp.where(tile == (iota + float(base + first)).astype(BF16), one, zero)
+        for first in range(0, count, 16)
+    ]
+    return jnp.concatenate(parts, axis=0) if len(parts) > 1 else parts[0]
+
+
+def bucket_kernel(slab_ref, cells_ref, moves_ref, accepted_ref, types_ref, msg_ref, own_ref, slot_ref,
+                  code, cls, dig_h, dig_l, one_y, one_s, ranked, prefix, left, right):
+    beads = cells_ref.shape[1]
+    chunks = beads // CHUNK
+    slab = slab_ref[0]
+    kind = types_ref[...] << 21
+
+    def moved(cell, step):
+        col_x = (cell + moves_ref[step, 0:1, :]) & (NX - 1)
+        row_y = ((cell >> 9) + moves_ref[step, 1:2, :]) & (NY - 1)
+        plane = ((cell >> 15) + moves_ref[step, 2:3, :]) & (ZDEV * GROUPS - 1)
+        return col_x | (row_y << 9) | (plane << 15)
+
+    start = cells_ref[...]
+    first = moved(start, 0)
+    after = jnp.where(accepted_ref[0:1, :] == 1, first, start)
+    second = moved(after, 1)
+    code[0:1, :] = start | kind
+    code[1:2, :] = after | kind
+    code[2:3, :] = first | kind
+    code[3:4, :] = second | kind
+    c = code[...]
+    block_y = (c >> 11) & 15
+    block_z = (c >> 17) & 15
+    row = ((c >> 9) & 3) * 4 + ((c >> 15) & 3)
+    high = ((c >> 7) & 3) * 32 + (c >> 21) * 16 + row
+    cls[0:SETS, :] = block_y.astype(F32)
+    cls[SETS : 2 * SETS, :] = block_z.astype(F32)
+    dig_h[...] = (high + 1).astype(F32)
+    dig_l[...] = (c & 127).astype(F32)
+    inside_all = jnp.where(block_z == slab, 1.0, 0.0)
+    cls[2 * SETS : 3 * SETS, :] = inside_all
+    for s in range(SETS):
+        y_hot = one_hot(cls[s : s + 1, :], 16)
+        one_y[s * 16 : s * 16 + 16, :] = y_hot
+        one_s[s * 16 : s * 16 + 16, :] = one_hot(cls[SETS + s : SETS + s + 1, :], 16)
+        inside = jnp.broadcast_to(cls[2 * SETS + s : 2 * SETS + s + 1, :], (16, beads)).astype(BF16)
+        mask = y_hot * inside
+        left[s * 32 : s * 32 + 16, :] = mask * jnp.broadcast_to(dig_h[s : s + 1, :], (16, beads)).astype(BF16)
+        left[s * 32 + 16 : s * 32 + 32, :] = mask * jnp.broadcast_to(dig_l[s : s + 1, :], (16, beads)).astype(BF16)
+        for k in range(chunks):
+            at = (s * chunks + k) * 16
+            ranked[at : at + 16, :] = mask[:, k * CHUNK : (k + 1) * CHUNK]
+    counts = lax.dot_general(one_s[...], one_y[...], CONTRACT_LANES, preferred_element_type=F32)
+    same = (
+        lax.broadcasted_iota(jnp.int32, counts.shape, 0) // 16
+        == lax.broadcasted_iota(jnp.int32, counts.shape, 1) // 16
+    )
+    largest = jnp.max(jnp.where(same, counts, 0.0))
+    over = jnp.where(largest > float(SLOTS), 1.0, 0.0)
+    rows = lax.broadcasted_iota(jnp.int32, (CHUNK, CHUNK + 128), 0)
+    cols = lax.broadcasted_iota(jnp.int32, (CHUNK, CHUNK + 128), 1)
+    upto = jnp.where((rows <= cols) | (cols >= CHUNK), 1.0, 0.0).astype(BF16)
+    prefix[...] = jnp.dot(ranked[...], upto, preferred_element_type=F32)
+    for s in range(SETS):
+        carry = jnp.zeros((16, 128), F32)
+        for k in range(chunks):
+            at = (s * chunks + k) * 16
+            mine = ranked[at : at + 16, :].astype(F32)
+            ahead = prefix[at : at + 16, 0:CHUNK] + jnp.concatenate([carry, carry], axis=1)
+            rank = jnp.sum(mine * ahead, axis=0, keepdims=True) - 1.0
+            carry = carry + prefix[at : at + 16, CHUNK : CHUNK + 128]
+            lanes = slice(k * CHUNK, (k + 1) * CHUNK)
+            right[:, lanes] = one_hot(rank, SLOTS)
+            slot_ref[s : s + 1, lanes] = jnp.where(rank >= 0.0, cls[s : s + 1, lanes] * SLOTS + rank, -1.0).astype(jnp.int32)
+        own_ref[s * 32 : s * 32 + 32, :] = lax.dot_general(
+            left[s * 32 : s * 32 + 32, :], right[...], CONTRACT_LANES, preferred_element_type=F32
+        ).astype(BF16)
+    for j in range(GROUPS):
+        msg_ref[j, 0:64, :] = own_ref[0:64, :]
+        msg_ref[j, 64:MSG, :] = jnp.broadcast_to(over, (MSG - 64, SLOTS)).astype(BF16)
+
+
+def bucket(slab, cells, moves, accepted, types):
+    beads = cells.shape[0]
+    vmem = pl.BlockSpec(memory_space=pltpu.VMEM)
+    return pl.pallas_call(
+        bucket_kernel,
+        out_shape=(
+            jax.ShapeDtypeStruct((GROUPS, MSG, SLOTS), BF16),
+            jax.ShapeDtypeStruct((SETS * 32, SLOTS), BF16),
+            jax.ShapeDtypeStruct((SETS, beads), jnp.int32),
+        ),
+        in_specs=[pl.BlockSpec(memory_space=pltpu.SMEM)] + [vmem] * 4,
+        out_specs=(vmem, vmem, vmem),
+        scratch_shapes=[
+            pltpu.VMEM((SETS, beads), jnp.int32),
+            pltpu.VMEM((3 * SETS, beads), F32),
+            pltpu.VMEM((SETS, beads), F32),
+            pltpu.VMEM((SETS, beads), F32),
+            pltpu.VMEM((SETS * 16, beads), BF16),
+            pltpu.VMEM((SETS * 16, beads), BF16),
+            pltpu.VMEM((SETS * beads // CHUNK * 16, CHUNK), BF16),
+            pltpu.VMEM((SETS * beads // CHUNK * 16, CHUNK + 128), F32),
+            pltpu.VMEM((SETS * 32, beads), BF16),
+            pltpu.VMEM((SLOTS, beads), BF16),
+        ],
+        name="bucket",
+    )(slab, cells.reshape(1, beads), moves, accepted, types.reshape(1, beads))
+
+
+def field_kernel(scale, place_ref, msg_ref, own_ref, slot_ref, table_ref, field_ref, change_ref,
+                 hot_h, hot_l, count_lo, count_hi, field, values):
+    def count_block(step, block):
+        for j in range(GROUPS):
+            lanes = slice(j * SLOTS, (j + 1) * SLOTS)
+            hot_h[:, lanes] = one_hot(msg_ref[j, pl.ds(step * 32 + block, 1), :].astype(F32), 128, 1)
+            hot_l[:, lanes] = one_hot(msg_ref[j, pl.ds(step * 32 + 16 + block, 1), :].astype(F32), 128)
+        hist = lax.dot_general(hot_h[...], hot_l[...], CONTRACT_LANES, preferred_element_type=F32)
+        high = jnp.floor(hist * (1.0 / 256.0))
+        low = hist - 256.0 * high
+        at = pl.multiple_of((step * GROUPS + block) * 32, 32)
+        for q in range(4):
+            count_lo[pl.ds(at, 32), q * 128 : (q + 1) * 128] = low[q * 32 : (q + 1) * 32, :].astype(BF16)
+            count_hi[pl.ds(at, 32), q * 128 : (q + 1) * 128] = high[q * 32 : (q + 1) * 32, :].astype(BF16)
+
+    for step in range(STEPS):
+        for block in range(GROUPS):
+            count_block(step, block)
+    table = table_ref[...]
+    for step in range(STEPS):
+        at = step * GROUPS * 32
+        rows = GROUPS * 32
+        dens = jnp.dot(count_lo[at : at + rows, :], table, preferred_element_type=F32)
+        dens += 256.0 * jnp.dot(count_hi[at : at + rows, :], table, preferred_element_type=F32)
+        dens = dens * scale
+        for block in range(GROUPS):
+            phi_a = dens[block * 32 : block * 32 + 16, :]
+            phi_b = dens[block * 32 + 16 : block * 32 + 32, :]
+            excess = kappa_comp * (phi_a + phi_b - 1.0)
+            field[at + block * 32 : at + block * 32 + 16, :] = (chi_mix * phi_b + excess).astype(BF16)
+            field[at + block * 32 + 16 : at + block * 32 + 32, :] = (chi_mix * phi_a + excess).astype(BF16)
+    mine = pl.multiple_of(((STEPS - 1) * GROUPS + place_ref[0]) * 32, 32)
+    field_ref[:, 0:NX] = field[pl.ds(mine, 16), :]
+    field_ref[:, NX : 2 * NX] = field[pl.ds(mine + 16, 16), :]
+    for step in range(STEPS):
+        for block in range(GROUPS):
+            at = (step * GROUPS + block) * 32
+            cells = jnp.concatenate([field[at : at + 32, q * 128 : (q + 1) * 128] for q in range(4)], axis=0)
+            hots, lows = [], []
+            for s in (step, STEPS + step):
+                hots.append(one_hot(own_ref[s * 32 + block : s * 32 + block + 1, :].astype(F32), 128, 1))
+                low = jnp.broadcast_to(own_ref[s * 32 + 16 + block : s * 32 + 17 + block, :].astype(F32), (128, SLOTS))
+                lows.append(low)
+            picked = lax.dot_general(
+                cells, jnp.concatenate(hots, axis=1), CONTRACT_SUBLANES, preferred_element_type=F32
+            )
+            lanes = lax.broadcasted_iota(jnp.int32, (128, 2 * SLOTS), 0).astype(F32)
+            chosen = jnp.where(jnp.concatenate(lows, axis=1) == lanes, picked, 0.0)
+            got = jnp.sum(chosen, axis=0, keepdims=True)
+            values[step * 32 + block : step * 32 + block + 1, :] = got[:, 0:SLOTS]
+            values[step * 32 + 16 + block : step * 32 + 17 + block, :] = got[:, SLOTS:]
+    for step in range(STEPS):
+        back = []
+        for which in range(2):
+            slot = slot_ref[which * STEPS + step]
+            rank = slot & (SLOTS - 1)
+            home = slot >> 7
+            total = jnp.zeros(slot.shape, F32)
+            for block in range(GROUPS):
+                at = step * 32 + which * 16 + block
+                line = jnp.broadcast_to(values[at : at + 1, :], slot.shape)
+                total = jnp.where(home == block, jnp.take_along_axis(line, rank, axis=1), total)
+            back.append(total)
+        change = (back[1] - back[0]).astype(BF16)
+        for j in range(GROUPS):
+            change_ref[j, step] = change
+
+
+def fields_and_changes(scale, place, msg, own, slot, table):
+    rows = slot.shape[1]
+    vmem = pl.BlockSpec(memory_space=pltpu.VMEM)
+    return pl.pallas_call(
+        functools.partial(field_kernel, scale),
+        out_shape=(
+            jax.ShapeDtypeStruct((16, 2 * NX), BF16),
+            jax.ShapeDtypeStruct((GROUPS, STEPS, rows, 128), BF16),
+        ),
+        in_specs=[pl.BlockSpec(memory_space=pltpu.SMEM)] + [vmem] * 4,
+        out_specs=(vmem, vmem),
+        scratch_shapes=[
+            pltpu.VMEM((128, GROUPS * SLOTS), BF16),
+            pltpu.VMEM((128, GROUPS * SLOTS), BF16),
+            pltpu.VMEM((STEPS * GROUPS * 32, NX), BF16),
+            pltpu.VMEM((STEPS * GROUPS * 32, NX), BF16),
+            pltpu.VMEM((STEPS * GROUPS * 32, NX), BF16),
+            pltpu.VMEM((STEPS * 32, SLOTS), F32),
+        ],
+        name="fields",
+    )(place, msg, own, slot, table)
+
+
+def local(cells_start, moves, accepted, bead_types):
+    beads = cells_start.shape[0]
+    slab = lax.axis_index("grid").astype(jnp.int32).reshape(1)
+    place = lax.axis_index("mol").astype(jnp.int32).reshape(1)
+    scale = NX * NY * ZDEV * GROUPS / (beads * GROUPS)
+    msg, own, slot = bucket(slab, cells_start, moves, accepted, bead_types)
+    msg = lax.all_to_all(msg, "mol", split_axis=0, concat_axis=0, tiled=True)
+    crowded = jnp.max(msg[:, 64, 0].astype(F32)) > 0.5
+
+    def bucketed(msg, own, slot, *_):
+        table = kernel_rows(jnp.arange(NX, dtype=jnp.int32))
+        field, change = fields_and_changes(scale, place, msg, own, slot.reshape(SETS, beads // 128, 128), table)
+        arrived = lax.all_to_all(change, "grid", split_axis=0, concat_axis=0, tiled=True)
+        total = arrived.astype(F32).sum(axis=0).reshape(STEPS, beads)
+        return total, field.reshape(4, ZDEV, 2 * NX)
+
+    def general(msg, own, slot, *arguments):
+        return any_spread(*arguments)
+
+    return lax.cond(crowded, general, bucketed, msg, own, slot, cells_start, moves, accepted, bead_types)
+
+
 def solution(mesh):
     return jax.shard_map(
         local,

time: 378 us -> 70 us (0.19)
  local copies, waits for them, and re-layouts: 212 us -> 3.86 us
  other arithmetic: 51.5 us -> 3.2 us
  matrix products: 29.3 us -> 0 us
  starting transfers between devices: 38.9 us -> 16.4 us
  Pallas kernels: 0 us -> 20.5 us
  waiting for transfers between devices: 42.4 us -> 24.1 us
    gather x4 -> x0, local copies, waits for them, and re-layouts: 202 us -> none  [read_beads(): picked = jnp.take(flat_table, flat_index).astype(jnp.float32)]
    select_n x18 -> x0, other arithmetic: 31.1 us -> none  [the longest x16 29.8 us: add_block(): first = jnp.where(types_here[:, None] == 0, spread_rows, zeros_bf)]
    dot_general x16 -> x0, matrix products: 29.3 us -> none  [add_block(): return total + jnp.dot(onehot, columns, preferred_element_type=jnp.float32)]
    all_to_all x6 -> x2, starting transfers between devices: 38.9 us -> 16.4 us  [the longest x1 10.9 us: bucketed(): lax.all_to_all(change, 'grid', split_axis=0, concat_axis=0, tiled=True)]
    pallas_call x0 -> x2, Pallas kernels: none -> 20.5 us  [the longest x1 14.8 us: fields_and_changes(): pl.pallas_call(functools.partial(field_kernel, scale), out_shape=(jax.Sha...]
    all_to_all x6 -> x2, waiting for transfers between devices: 42.4 us -> 24.1 us  [the longest x1 15.4 us: bucketed(): lax.all_to_all(change, 'grid', split_axis=0, concat_axis=0, tiled=True)]
    reduce_sum x16 -> x1, other arithmetic: 9.9 us -> 0.62 us  [kernel_rows(): total = jnp.sum(jnp.exp(-first * first / (2.0 * SPREAD * SPREAD)))]
    eq x17 -> x0, other arithmetic: 6.56 us -> none  [the longest x16 5.61 us: add_block(): first = jnp.where(types_here[:, None] == 0, spread_rows, zeros_bf)]
  transfers between devices with their start and end apart: 6 -> 2, of which waited for: 3 -> 2; matrix products, arithmetic and copies ran while one was open for 67% -> 1% of each run, Pallas kernels for 0% -> 0%
where the time goes in v1:
time: 70 us; the launch traced here: 69.6 us
  waiting for transfers between devices  24.1 us (34%)
  Pallas kernels  20.5 us (29%)
  starting transfers between devices  16.4 us (23%)
  local copies, waits for them, and re-layouts  3.86 us (6%)
  other arithmetic  3.2 us (5%)
  between operations  1.37 us (2%)
    all_to_all x1, waiting for transfers between devices, bucketed(): lax.all_to_all(change, 'grid', split_axis=0, concat_axis=0, tiled=True)  15.4 us
    pallas_call x1, Pallas kernels, fields_and_changes(): pl.pallas_call(functools.partial(field_kernel, scale), out_shape=(jax.Sha...  14.8 us
    all_to_all x1, starting transfers between devices, bucketed(): lax.all_to_all(change, 'grid', split_axis=0, concat_axis=0, tiled=True)  10.9 us
    all_to_all x1, waiting for transfers between devices, local(): msg = lax.all_to_all(msg, 'mol', split_axis=0, concat_axis=0, tiled=True)  8.71 us
    pallas_call x1, Pallas kernels, bucket(): pl.pallas_call(bucket_kernel, out_shape=(jax.ShapeDtypeStruct((GROUPS, MS...  5.69 us
    all_to_all x1, starting transfers between devices, local(): msg = lax.all_to_all(msg, 'mol', split_axis=0, concat_axis=0, tiled=True)  5.5 us
    convert_element_type x1, other arithmetic, kernel_rows(): return (weights / total).astype(jnp.bfloat16)  1.88 us
    unnamed x9, local copies, waits for them, and re-layouts  1.87 us
  transfers between devices with their start and end apart: 2, of which 2 were waited for; matrix products, arithmetic and copies ran while one was open for 1% of the time, Pallas kernels for 0%

profile of v1, /device:TPU:32, one launch (start us, length us, event | category | flops | bytes accessed | tf_op | source)
XLA Modules:
  0.0 69.6 jit_solution(2094243537950626046)
XLA Ops:
  0.6 0.0 copy-start
  0.6 0.0 copy-start.1
  0.7 0.0 copy-start.3
  0.7 0.0 copy-start.2
  0.7 1.8 %copy.22.moves_ref = s32[2,3,8192]{2,1,0:T(4,128)} copy(s32[2,3,8192]{2,0,1:T(2,128)} %param.13) | data formatting | bytes 393216 | tf_op args[1]
  2.5 5.7 %bucket.1 = (bf16[16,80,128]{2,1,0:T(8,128)(2,1)}, bf16[128,128]{1,0:T(8,128)(2,1)S(1)}, s32[4,8192]{1,0:T(4,128)S(1)}) custom-call(s32[1]{0:T(128)} %bitcast.11.slab_ref, s32[1,8192]{1,0:T(1,128)} %bitcast.36, s32[2,3,8192]{2,1,0:T(4,128)} %copy.22.moves_ref, s32[2,8192]{1,0:T(2,128)} %accepted_ref.1, s32[1,8192]{1,0:T(1,128)} %bitcast.42), custom_call_target="tpu_custom_call" | custom-call | tf_op jit(solution)/shard_map/bucket/pallas_call | solution.py:262
  8.2 5.5 %all-to-all-start.7 = ((bf16[16,80,128]{2,1,0:T(8,128)(2,1)}), bf16[16,80,128]{2,1,0:T(8,128)(2,1)S(1)}, u32[]{:S(2)}, u32[]{:S(2)}) async-start(bf16[16,80,128]{2,1,0:T(8,128)(2,1)} %get-tuple-element.251), calls=%async_computation.7 | async-start | bytes 655360 | tf_op jit(solution)/shard_map/all_to_all | solution.py:384
  13.7 8.7 %all-to-all-done.7 = bf16[16,80,128]{2,1,0:T(8,128)(2,1)S(1)} async-done(((bf16[16,80,128]{2,1,0:T(8,128)(2,1)}), bf16[16,80,128]{2,1,0:T(8,128)(2,1)S(1)}, u32[]{:S(2)}, u32[]{:S(2)}) %all-to-all-start.7) | async-done | bytes 327712 | tf_op jit(solution)/shard_map/all_to_all | solution.py:384
  22.4 0.6 slice_reduce_fusion
  23.7 0.0 copy-done
  23.7 0.0 copy-done.1
  23.7 0.0 copy-done.3
  23.7 0.0 copy-done.2
  23.8 45.8 %conditional.1 = (f32[2,8192]{1,0:T(2,128)}, bf16[4,4,1024]{2,1,0:T(4,128)(2,1)}) conditional(s32[]{:T(128)} %convert_element_type.71, (s32[]{:T(128)}, s32[4,8192]{1,0:T(4,128)S(1)}, bf16[16,80,128]{2,1,0:T(8,128)(2,1)S(1)}, bf16[128,128]{1,0:T(8,128)(2,1)S(1)}) %tuple.44, (s32[8192]{0:T(1024)S(1)}, s32[2,3,8192]{2,0,1:T(2,128)S(1)}, ...), branch_computations={%region_1.0_spmd, %region_4.16_spmd} | conditional | flops 1102073856 | bytes 41468720 | solution.py:397
  24.0 0.6 fusion.10
  24.6 0.7 copy.34
  25.2 1.9 %fusion.7.table_ref = bf16[512,512]{1,0:T(8,128)(2,1)} fusion(f32[]{:T(128)} %fusion.10, f32[512]{0:T(512)S(1)} %iota_convert_fusion), kind=kLoop, calls=%fused_computation.10 | loop fusion | flops 2359296 | bytes 526340 | tf_op jit(solution)/shard_map/cond/branch_0_fun/convert_element_type | solution.py:69
  27.1 14.8 %fields.1 = (bf16[16,1024]{1,0:T(8,128)(2,1)}, bf16[16,2,64,128]{3,2,1,0:T(8,128)(2,1)}) custom-call(s32[1]{0:T(128)} %bitcast.place_ref, bf16[16,80,128]{2,1,0:T(8,128)(2,1)S(1)} %get-tuple-element.221.msg_ref, bf16[128,128]{1,0:T(8,128)(2,1)S(1)} %get-tuple-element.222.own_ref, s32[4,64,128]{2,1,0:T(8,128)} %bitcast.41, bf16[512,512]{1,0:T(8,128)(2,1)} %fusion.7.table_ref), custom_call_target="tpu_custom_call" | custom-call | tf_op jit(solution)/shard_map/cond/branch_0_fun/fields/pallas_call | solution.py:358
  41.9 10.9 %all-to-all-start = ((bf16[16,2,64,128]{3,2,1,0:T(8,128)(2,1)}), bf16[16,2,64,128]{3,2,1,0:T(8,128)(2,1)S(1)}, u32[]{:S(2)}, u32[]{:S(2)}) async-start(bf16[16,2,64,128]{3,2,1,0:T(8,128)(2,1)} %get-tuple-element.224), calls=%async_computation | async-start | bytes 1048576 | tf_op jit(solution)/shard_map/cond/branch_0_fun/all_to_all | solution.py:390
  52.8 0.0 copy-done.5
  52.8 0.6 reshape.66
  53.4 15.4 %all-to-all-done = bf16[16,2,64,128]{3,2,1,0:T(8,128)(2,1)S(1)} async-done(((bf16[16,2,64,128]{3,2,1,0:T(8,128)(2,1)}), bf16[16,2,64,128]{3,2,1,0:T(8,128)(2,1)S(1)}, u32[]{:S(2)}, u32[]{:S(2)}) %all-to-all-start) | async-done | bytes 524320 | tf_op jit(solution)/shard_map/cond/branch_0_fun/all_to_all | solution.py:390
  68.8 0.1 convert_reduce_fusion
  68.9 0.7 copy.35
  (2 shorter events, 0.0 us)
Async XLA Ops:
  0.6 23.1 %copy-start = (s32[2,3,8192]{2,0,1:T(2,128)S(1)}, s32[2,3,8192]{2,0,1:T(2,128)}, u32[]{:S(2)}) copy-start(s32[2,3,8192]{2,0,1:T(2,128)} %param.13) | copy-start | bytes 589828
  0.6 23.1 %copy-start.1 = (s32[8192]{0:T(1024)S(1)}, s32[8192]{0:T(1024)}, u32[]{:S(2)}) copy-start(s32[8192]{0:T(1024)} %param.12) | copy-start | bytes 98308
  0.7 23.1 %copy-start.3 = (s32[2,8192]{1,0:T(2,128)S(1)}, s32[2,8192]{1,0:T(2,128)}, u32[]{:S(2)}) copy-start(s32[2,8192]{1,0:T(2,128)} %accepted_ref.1) | copy-start | bytes 196612
  0.7 23.1 %copy-start.2 = (s32[8192]{0:T(1024)S(1)}, s32[8192]{0:T(1024)}, u32[]{:S(2)}) copy-start(s32[8192]{0:T(1024)} %param.15) | copy-start | bytes 98308
  8.2 14.2 %all-to-all-start.7 = ((bf16[16,80,128]{2,1,0:T(8,128)(2,1)}), bf16[16,80,128]{2,1,0:T(8,128)(2,1)S(1)}, u32[]{:S(2)}, u32[]{:S(2)}) async-start(bf16[16,80,128]{2,1,0:T(8,128)(2,1)} %get-tuple-element.251), calls=%async_computation.7 | async-start | bytes 655360 | tf_op jit(solution)/shard_map/all_to_all | solution.py:384
  41.9 10.9 %copy-start.5 = (bf16[16,1024]{1,0:T(8,128)(2,1)S(1)}, bf16[16,1024]{1,0:T(8,128)(2,1)}, u32[]{:S(2)}) copy-start(bf16[16,1024]{1,0:T(8,128)(2,1)} %get-tuple-element.225) | copy-start | bytes 98308 | tf_op jit(solution)/shard_map/cond
  41.9 26.9 %all-to-all-start = ((bf16[16,2,64,128]{3,2,1,0:T(8,128)(2,1)}), bf16[16,2,64,128]{3,2,1,0:T(8,128)(2,1)S(1)}, u32[]{:S(2)}, u32[]{:S(2)}) async-start(bf16[16,2,64,128]{3,2,1,0:T(8,128)(2,1)} %get-tuple-element.224), calls=%async_computation | async-start | bytes 1048576 | tf_op jit(solution)/shard_map/cond/branch_0_fun/all_to_all | solution.py:390

commit v2 on v0

--- a/solution.py
+++ b/solution.py
@@ -1,6 +1,10 @@
+import functools
+
 import jax
 import jax.numpy as jnp
 from jax import lax
+from jax.experimental import pallas as pl
+from jax.experimental.pallas import tpu as pltpu
 from jax.sharding import PartitionSpec as P
 
 NX = 512
@@ -8,6 +12,17 @@
 ZDEV = 4
 STEPS = 2
 SPREAD = 2
+SLABS = 16
+BANDS = 8
+SLOTS = 128
+CHUNK = 256
+BLOCK = 1024
+SETS = 4
+ROWS = NY * ZDEV
+MARK = 320.0
+F32 = jnp.float32
+BF16 = jnp.bfloat16
+LANES = (((1,), (1,)), ((), ()))
 
 
 chi_mix = 1.0
@@ -124,7 +139,7 @@
     return read_beads
 
 
-def local(cells_start, moves, accepted, bead_types):
+def any_spread(cells_start, moves, accepted, bead_types):
     grid_count = lax.axis_size("grid")
     mol_count = lax.axis_size("mol")
     slab = lax.axis_index("grid")
@@ -157,6 +172,318 @@
     return (jnp.stack(changes), fields[STEPS - 1])
 
 
+def one_hot(row, count, base=0):
+    width = row.shape[1]
+    tile = jnp.broadcast_to(row, (16, width)).astype(BF16)
+    iota = lax.broadcasted_iota(jnp.int32, (16, width), 0).astype(F32)
+    one = jnp.ones((16, width), BF16)
+    zero = jnp.zeros((16, width), BF16)
+    parts = [
+        jnp.where(tile == (iota + float(base + first)).astype(BF16), one, zero)
+        for first in range(0, count, 16)
+    ]
+    return jnp.concatenate(parts, axis=0) if len(parts) > 1 else parts[0]
+
+
+def prefix_matrix():
+    rows = lax.broadcasted_iota(jnp.int32, (CHUNK, CHUNK + 128), 0)
+    cols = lax.broadcasted_iota(jnp.int32, (CHUNK, CHUNK + 128), 1)
+    return jnp.where((rows <= cols) | (cols >= CHUNK), 1.0, 0.0).astype(BF16)
+
+
+def stacked(rows, width):
+    iota = lax.broadcasted_iota(jnp.int32, (16, width), 0)
+    total = jnp.zeros((16, width), F32)
+    for i, row in enumerate(rows):
+        total = jnp.where(iota == i, jnp.broadcast_to(row, (16, width)), total)
+    return total.astype(BF16)
+
+
+def bucket_kernel(slab_ref, cells_ref, moves_ref, accepted_ref, types_ref, msg_ref, code_ref,
+                  slabs, bands, highs, lows, ranked, prefix):
+    beads = cells_ref.shape[1]
+    chunks = beads // CHUNK
+    slab = slab_ref[0]
+    kind = types_ref[...] << 21
+
+    def moved(cell, step):
+        col_x = (cell + moves_ref[0, step : step + 1, :]) & (NX - 1)
+        row_y = ((cell >> 9) + moves_ref[1, step : step + 1, :]) & (NY - 1)
+        plane = ((cell >> 15) + moves_ref[2, step : step + 1, :]) & (ZDEV * SLABS - 1)
+        return col_x | (row_y << 9) | (plane << 15)
+
+    start = cells_ref[...]
+    first = moved(start, 0)
+    after = jnp.where(accepted_ref[0:1, :] == 1, first, start)
+    second = moved(after, 1)
+    code_ref[0:1, :] = start | kind
+    code_ref[1:2, :] = after | kind
+    code_ref[2:3, :] = first | kind
+    code_ref[3:4, :] = second | kind
+    c = code_ref[...]
+    slabs[...] = ((c >> 17) & 15).astype(F32)
+    band = (c >> 12) & 7
+    bands[0:SETS, :] = band.astype(F32)
+    bands[SETS : 2 * SETS, :] = jnp.where(((c >> 17) & 15) == slab, band, -64).astype(F32)
+    highs[...] = (((c >> 7) & 3) * 64 + (c >> 21) * 32 + ((c >> 9) & 7) * 4 + ((c >> 15) & 3) + 1).astype(F32)
+    lows[...] = (c & 127).astype(F32)
+    counts = jnp.zeros((SETS * 16, 32), F32)
+    upper = lax.broadcasted_iota(jnp.int32, (16, CHUNK), 0) >= BANDS
+    own_row = (lax.broadcasted_iota(jnp.int32, (16, CHUNK), 0) & (BANDS - 1)).astype(F32).astype(BF16)
+    one = jnp.ones((16, CHUNK), BF16)
+    zero = jnp.zeros((16, CHUNK), BF16)
+
+    def both(ref, base, lanes):
+        low = jnp.broadcast_to(ref[base : base + 1, lanes], (16, CHUNK))
+        high = jnp.broadcast_to(ref[base + 1 : base + 2, lanes], (16, CHUNK))
+        return jnp.where(upper, high, low).astype(BF16)
+
+    for k in range(chunks):
+        lanes = slice(k * CHUNK, (k + 1) * CHUNK)
+        of_slab = jnp.concatenate([one_hot(slabs[s : s + 1, lanes], 16) for s in range(SETS)], axis=0)
+        of_band = jnp.where(both(bands, 0, lanes) == own_row, one, zero)
+        block = one_hot(jnp.full((1, CHUNK), float(k * CHUNK // BLOCK), F32), 16)
+        counts += lax.dot_general(of_slab, jnp.concatenate([of_band, block], axis=0), LANES, preferred_element_type=F32)
+        ranked[k * 16 : k * 16 + 16, :] = jnp.where(both(bands, SETS, lanes) == own_row, one, zero)
+    set_of = lax.broadcasted_iota(jnp.int32, counts.shape, 0) // 16
+    column = lax.broadcasted_iota(jnp.int32, counts.shape, 1)
+    used = (column >= 16) | (set_of == column // BANDS)
+    crowded = jnp.max(jnp.where(used, counts, 0.0)) > float(SLOTS)
+    prefix[...] = jnp.dot(ranked[...], prefix_matrix(), preferred_element_type=F32)
+    carry = jnp.zeros((16, 128), F32)
+    out = [jnp.zeros((16, SLOTS), F32), jnp.zeros((16, SLOTS), F32)]
+    for k in range(chunks):
+        lanes = slice(k * CHUNK, (k + 1) * CHUNK)
+        mine = ranked[k * 16 : k * 16 + 16, :]
+        ahead = mine.astype(F32) * (prefix[k * 16 : k * 16 + 16, 0:CHUNK] + jnp.concatenate([carry, carry], axis=1))
+        carry = carry + prefix[k * 16 : k * 16 + 16, CHUNK : CHUNK + 128]
+        for s in range(STEPS):
+            rank = jnp.sum(ahead[s * BANDS : (s + 1) * BANDS, :], axis=0, keepdims=True) - 1.0
+            low = jnp.broadcast_to(lows[s : s + 1, lanes], (16, CHUNK))
+            high = jnp.broadcast_to(highs[s : s + 1, lanes], (16, CHUNK))
+            inside = jnp.broadcast_to(bands[SETS + s : SETS + s + 1, lanes], (16, CHUNK)).astype(BF16)
+            left = jnp.where(inside == own_row, jnp.where(upper, low, high).astype(BF16), zero)
+            out[s] += lax.dot_general(left, one_hot(rank, SLOTS), LANES, preferred_element_type=F32)
+    corner = (lax.broadcasted_iota(jnp.int32, (16, SLOTS), 0) == 0) & (
+        lax.broadcasted_iota(jnp.int32, (16, SLOTS), 1) == 0
+    )
+    out[0] = jnp.where(corner & crowded, MARK, out[0])
+    lists = jnp.concatenate(out, axis=0).astype(BF16)
+    for j in range(SLABS):
+        msg_ref[j] = lists
+
+
+def rank_kernel(slab_ref, code_ref, own_ref, slot_ref, slabs, digits, ranked, prefix):
+    beads = code_ref.shape[1]
+    chunks = beads // CHUNK
+    c = code_ref[...]
+    slabs[...] = ((c >> 17) & 15).astype(F32)
+    digits[0:SETS, :] = (((c >> 9) & 63) * 4 + ((c >> 15) & 3)).astype(F32)
+    digits[SETS : 2 * SETS, :] = ((c >> 21) * 2 + ((c >> 8) & 1) + 1).astype(F32)
+    digits[2 * SETS : 3 * SETS, :] = (c & 255).astype(F32)
+    here = slab_ref[0].astype(F32)
+    for s in range(SETS):
+        for k in range(chunks):
+            at = (s * chunks + k) * 16
+            ranked[at : at + 16, :] = one_hot(slabs[s : s + 1, k * CHUNK : (k + 1) * CHUNK], 16)
+    prefix[...] = jnp.dot(ranked[...], prefix_matrix(), preferred_element_type=F32)
+    for s in range(SETS):
+        for block in range(beads // BLOCK):
+            carry = jnp.zeros((16, 128), F32)
+            lists = jnp.zeros((16, SLOTS), F32)
+            for k in range(block * BLOCK // CHUNK, (block + 1) * BLOCK // CHUNK):
+                at = (s * chunks + k) * 16
+                lanes = slice(k * CHUNK, (k + 1) * CHUNK)
+                ahead = prefix[at : at + 16, 0:CHUNK] + jnp.concatenate([carry, carry], axis=1)
+                carry = carry + prefix[at : at + 16, CHUNK : CHUNK + 128]
+                rank = jnp.sum(ranked[at : at + 16, :].astype(F32) * ahead, axis=0, keepdims=True) - 1.0
+                home = slabs[s : s + 1, lanes]
+                slot = (home * float(SLOTS) + rank).astype(jnp.int32)
+                for i in range(CHUNK // 128):
+                    line = k * CHUNK // 128 + i
+                    slot_ref[s, line : line + 1, :] = slot[:, i * 128 : (i + 1) * 128]
+                held = jnp.where(home == here, rank, -1.0)
+                left = stacked([digits[d * SETS + s : d * SETS + s + 1, lanes] for d in range(3)], CHUNK)
+                lists += lax.dot_general(left, one_hot(held, SLOTS), LANES, preferred_element_type=F32)
+            at = (s * (beads // BLOCK) + block) * 8
+            own_ref[at : at + 8, :] = lists[0:8, :]
+
+
+def field_kernel(scale, place_ref, msg_ref, own_ref, table_ref, field_ref, value_ref,
+                 count_lo, count_hi, field, values):
+    blocks = own_ref.shape[0] // (8 * SETS)
+    half = ROWS * 2
+    for step in range(STEPS):
+        for band in range(BANDS):
+            hist = jnp.zeros((256, SLOTS), F32)
+            for j in range(0, SLABS, 2):
+                at = step * 16 + band
+                high = [msg_ref[i, at : at + 1, :].astype(F32) for i in (j, j + 1)]
+                low = [msg_ref[i, at + BANDS : at + BANDS + 1, :].astype(F32) for i in (j, j + 1)]
+                hist += lax.dot_general(
+                    one_hot(jnp.concatenate(high, axis=1), 256, 1),
+                    one_hot(jnp.concatenate(low, axis=1), 128),
+                    LANES,
+                    preferred_element_type=F32,
+                )
+            upper = jnp.floor(hist * (1.0 / 256.0))
+            lower = hist - 256.0 * upper
+            for q in range(4):
+                for t in range(2):
+                    at = step * half + t * ROWS + band * 32
+                    rows = slice(q * 64 + t * 32, q * 64 + t * 32 + 32)
+                    count_lo[at : at + 32, q * 128 : (q + 1) * 128] = lower[rows, :].astype(BF16)
+                    count_hi[at : at + 32, q * 128 : (q + 1) * 128] = upper[rows, :].astype(BF16)
+
+    def mixed(phi_a, phi_b):
+        excess = kappa_comp * (phi_a + phi_b - 1.0)
+        return (chi_mix * phi_b + excess).astype(BF16), (chi_mix * phi_a + excess).astype(BF16)
+
+    table = table_ref[...]
+    for step in range(STEPS):
+        rows = slice(step * half, (step + 1) * half)
+        dens = lax.dot_general(table, count_lo[rows, :], LANES, preferred_element_type=F32)
+        dens += 256.0 * lax.dot_general(table, count_hi[rows, :], LANES, preferred_element_type=F32)
+        dens = dens * scale
+        field_a, field_b = mixed(dens[:, 0:ROWS], dens[:, ROWS:])
+        field[step, :, 0:ROWS] = field_a
+        field[step, :, ROWS:] = field_b
+    at = (STEPS - 1) * half + place_ref[0] * 16
+    mine = []
+    for t in range(2):
+        rows = pl.ds(pl.multiple_of(at + t * ROWS, 16), 16)
+        dens = jnp.dot(count_lo[rows, :], table, preferred_element_type=F32)
+        dens += 256.0 * jnp.dot(count_hi[rows, :], table, preferred_element_type=F32)
+        mine.append(dens * scale)
+    for t, part in enumerate(mixed(*mine)):
+        for y in range(4):
+            field_ref[y, :, t * NX : (t + 1) * NX] = part[y * ZDEV : (y + 1) * ZDEV, :]
+    column = lax.broadcasted_iota(jnp.int32, (256, CHUNK), 0).astype(F32)
+    for step in range(STEPS):
+        for which in range(2):
+            for block in range(0, blocks, 2):
+                at = ((which * STEPS + step) * blocks + block) * 8
+
+                def digit(d):
+                    return jnp.concatenate([own_ref[at + d : at + d + 1, :], own_ref[at + 8 + d : at + 9 + d, :]], axis=1)
+
+                row, part, low = digit(0), digit(1), digit(2)
+                picked = jnp.zeros((256, CHUNK), F32)
+                for q in range(4):
+                    x_at, t_at = (q & 1) * 256, (q >> 1) * ROWS
+                    picked += jnp.dot(
+                        field[step, x_at : x_at + 256, t_at : t_at + ROWS],
+                        one_hot(jnp.where(part == q + 1.0, row, -1.0), ROWS),
+                        preferred_element_type=F32,
+                    )
+                got = jnp.sum(jnp.where(column == low, picked, 0.0), axis=0, keepdims=True)
+                to = (step * 2 + which) * blocks + block
+                values[to : to + 1, :] = got[:, 0:SLOTS]
+                values[to + 1 : to + 2, :] = got[:, SLOTS:]
+    lists = values[...].astype(BF16)
+    for j in range(SLABS):
+        value_ref[j] = lists
+
+
+def change_kernel(value_ref, slot_ref, field_in_ref, change_ref, field_ref):
+    lines = slot_ref.shape[1]
+    blocks = lines * 128 // BLOCK
+    for step in range(STEPS):
+        for block in range(blocks):
+            back = []
+            for which in range(2):
+                slot = slot_ref[which * STEPS + step, block * 8 : block * 8 + 8, :]
+                rank = slot & (SLOTS - 1)
+                home = slot >> 7
+                at = (step * 2 + which) * blocks + block
+                total = jnp.zeros((8, 128), F32)
+                for j in range(SLABS):
+                    line = jnp.broadcast_to(value_ref[j, at : at + 1, :].astype(F32), (8, 128))
+                    total = jnp.where(home == j, jnp.take_along_axis(line, rank, axis=1), total)
+                back.append(total)
+            change = back[1] - back[0]
+            for i in range(8):
+                lanes = slice((block * 8 + i) * 128, (block * 8 + i + 1) * 128)
+                change_ref[step : step + 1, lanes] = change[i : i + 1, :]
+    field_ref[...] = field_in_ref[...]
+
+
+VMEM = pl.BlockSpec(memory_space=pltpu.VMEM)
+SMEM = pl.BlockSpec(memory_space=pltpu.SMEM)
+
+
+def shape(dims, dtype):
+    return jax.ShapeDtypeStruct(dims, dtype)
+
+
+def local(cells_start, moves, accepted, bead_types):
+    beads = cells_start.shape[0]
+    chunks = beads // CHUNK
+    blocks = beads // BLOCK
+    slab = lax.axis_index("grid").astype(jnp.int32).reshape(1)
+    place = lax.axis_index("mol").astype(jnp.int32).reshape(1)
+    scale = NX * NY * ZDEV * SLABS / (beads * lax.axis_size("mol"))
+    msg, code = pl.pallas_call(
+        bucket_kernel,
+        out_shape=(shape((SLABS, 32, SLOTS), BF16), shape((SETS, beads), jnp.int32)),
+        in_specs=[SMEM] + [VMEM] * 4,
+        out_specs=(VMEM, VMEM),
+        scratch_shapes=[
+            pltpu.VMEM((SETS, beads), F32),
+            pltpu.VMEM((2 * SETS, beads), F32),
+            pltpu.VMEM((SETS, beads), F32),
+            pltpu.VMEM((SETS, beads), F32),
+            pltpu.VMEM((chunks * 16, CHUNK), BF16),
+            pltpu.VMEM((chunks * 16, CHUNK + 128), F32),
+        ],
+        name="bucket",
+    )(slab, cells_start.reshape(1, beads), jnp.moveaxis(moves, 1, 0), accepted, bead_types.reshape(1, beads))
+    msg = lax.all_to_all(msg, "mol", split_axis=0, concat_axis=0, tiled=True)
+    own, slot = pl.pallas_call(
+        rank_kernel,
+        out_shape=(shape((SETS * blocks * 8, SLOTS), F32), shape((SETS, beads // 128, 128), jnp.int32)),
+        in_specs=[SMEM, VMEM],
+        out_specs=(VMEM, VMEM),
+        scratch_shapes=[
+            pltpu.VMEM((SETS, beads), F32),
+            pltpu.VMEM((3 * SETS, beads), F32),
+            pltpu.VMEM((SETS * chunks * 16, CHUNK), BF16),
+            pltpu.VMEM((SETS * chunks * 16, CHUNK + 128), F32),
+        ],
+        name="ranks",
+    )(slab, code)
+    table = kernel_rows(jnp.arange(NX, dtype=jnp.int32))
+    field, value = pl.pallas_call(
+        functools.partial(field_kernel, scale),
+        out_shape=(shape((4, ZDEV, 2 * NX), BF16), shape((SLABS, SETS * blocks, SLOTS), BF16)),
+        in_specs=[SMEM] + [VMEM] * 3,
+        out_specs=(VMEM, VMEM),
+        scratch_shapes=[
+            pltpu.VMEM((STEPS * ROWS * 2, NX), BF16),
+            pltpu.VMEM((STEPS * ROWS * 2, NX), BF16),
+            pltpu.VMEM((STEPS, NX, ROWS * 2), BF16),
+            pltpu.VMEM((SETS * blocks, SLOTS), F32),
+        ],
+        name="fields",
+    )(place, msg, own, table)
+    value = lax.all_to_all(value, "grid", split_axis=0, concat_axis=0, tiled=True)
+    crowded = jnp.max(msg[:, 0, 0].astype(F32)) >= MARK
+
+    def bucketed(value, slot, field, *_):
+        return pl.pallas_call(
+            change_kernel,
+            out_shape=(shape((STEPS, beads), F32), shape(field.shape, BF16)),
+            in_specs=[VMEM] * 3,
+            out_specs=(VMEM, VMEM),
+            name="changes",
+        )(value, slot, field)
+
+    def general(value, slot, field, *arguments):
+        return any_spread(*arguments)
+
+    return lax.cond(crowded, general, bucketed, value, slot, field, cells_start, moves, accepted, bead_types)
+
+
 def solution(mesh):
     return jax.shard_map(
         local,

time: 378 us -> 52.3 us (0.14)
  local copies, waits for them, and re-layouts: 212 us -> 1.31 us
  other arithmetic: 51.5 us -> 3.87 us
  waiting for transfers between devices: 42.4 us -> 7.98 us
  matrix products: 29.3 us -> 0 us
  starting transfers between devices: 38.9 us -> 16.4 us
  Pallas kernels: 0 us -> 20.2 us
    gather x4 -> x0, local copies, waits for them, and re-layouts: 202 us -> none  [read_beads(): picked = jnp.take(flat_table, flat_index).astype(jnp.float32)]
    all_to_all x6 -> x2, waiting for transfers between devices: 42.4 us -> 7.98 us  [the longest x1 7.97 us: local(): lax.all_to_all(value, 'grid', split_axis=0, concat_axis=0, tiled=True)]
    select_n x18 -> x0, other arithmetic: 31.1 us -> none  [the longest x16 29.8 us: add_block(): first = jnp.where(types_here[:, None] == 0, spread_rows, zeros_bf)]
    dot_general x16 -> x0, matrix products: 29.3 us -> none  [add_block(): return total + jnp.dot(onehot, columns, preferred_element_type=jnp.float32)]
    all_to_all x6 -> x2, starting transfers between devices: 38.9 us -> 16.4 us  [the longest x1 10.7 us: local(): lax.all_to_all(value, 'grid', split_axis=0, concat_axis=0, tiled=True)]
    pallas_call x0 -> x4, Pallas kernels: none -> 20.2 us  [the longest x1 10.1 us: local(): pl.pallas_call(functools.partial(field_kernel, scale), out_shape=(shape((...]
    reduce_sum x16 -> x1, other arithmetic: 9.9 us -> 0.62 us  [kernel_rows(): total = jnp.sum(jnp.exp(-first * first / (2.0 * SPREAD * SPREAD)))]
    eq x17 -> x0, other arithmetic: 6.56 us -> none  [the longest x16 5.61 us: add_block(): first = jnp.where(types_here[:, None] == 0, spread_rows, zeros_bf)]
  transfers between devices with their start and end apart: 6 -> 2, of which waited for: 3 -> 1; matrix products, arithmetic and copies ran while one was open for 67% -> 8% of each run, Pallas kernels for 0% -> 9%
where the time goes in v2:
time: 52.3 us; the launch traced here: 51.3 us
  Pallas kernels  20.2 us (39%)
  starting transfers between devices  16.4 us (31%)
  waiting for transfers between devices  7.98 us (15%)
  other arithmetic  3.87 us (7%)
  between operations  1.33 us (3%)
  local copies, waits for them, and re-layouts  1.31 us (3%)
    all_to_all x1, starting transfers between devices, local(): lax.all_to_all(value, 'grid', split_axis=0, concat_axis=0, tiled=True)  10.7 us
    pallas_call x1, Pallas kernels, local(): pl.pallas_call(functools.partial(field_kernel, scale), out_shape=(shape((...  10.1 us
    all_to_all x1, waiting for transfers between devices, local(): lax.all_to_all(value, 'grid', split_axis=0, concat_axis=0, tiled=True)  7.97 us
    all_to_all x1, starting transfers between devices, local(): msg = lax.all_to_all(msg, 'mol', split_axis=0, concat_axis=0, tiled=True)  5.65 us
    pallas_call x1, Pallas kernels, local(): pl.pallas_call(rank_kernel, out_shape=(shape((SETS * blocks * 8, SLOTS),...  4.71 us
    pallas_call x1, Pallas kernels, local(): pl.pallas_call(bucket_kernel, out_shape=(shape((SLABS, 32, SLOTS), BF16),...  4.23 us
    convert_element_type x1, other arithmetic, kernel_rows(): return (weights / total).astype(jnp.bfloat16)  1.87 us
    reduce_max x1, other arithmetic, local(): crowded = jnp.max(msg[:, 0, 0].astype(F32)) >= MARK  1.38 us
  transfers between devices with their start and end apart: 2, of which 1 were waited for; matrix products, arithmetic and copies ran while one was open for 8% of the time, Pallas kernels for 9%

profile of v2, /device:TPU:32, one launch (start us, length us, event | category | flops | bytes accessed | tf_op | source)
XLA Modules:
  0.0 51.3 jit_solution(1245159828814507029)
XLA Ops:
  0.6 4.2 %bucket.1 = (bf16[16,32,128]{2,1,0:T(8,128)(2,1)}, s32[4,8192]{1,0:T(4,128)}) custom-call(s32[1]{0:T(128)} %bitcast.10.slab_ref, s32[1,8192]{1,0:T(1,128)} %bitcast.30, s32[3,2,8192]{2,1,0:T(2,128)} %bitcast.27, s32[2,8192]{1,0:T(2,128)} %accepted_ref.1, s32[1,8192]{1,0:T(1,128)} %bitcast.35), custom_call_target="tpu_custom_call" | custom-call | tf_op jit(solution)/shard_map/bucket/pallas_call | solution.py:426
  4.9 0.0 copy-start
  4.9 0.0 copy-start.2
  4.9 0.0 copy-start.3
  4.9 0.0 copy-start.4
  4.9 5.6 %all-to-all-start.6 = ((bf16[16,32,128]{2,1,0:T(8,128)(2,1)}), bf16[16,32,128]{2,1,0:T(8,128)(2,1)S(1)}, u32[]{:S(2)}, u32[]{:S(2)}) async-start(bf16[16,32,128]{2,1,0:T(8,128)(2,1)} %get-tuple-element.248), calls=%async_computation.6 | async-start | bytes 262144 | tf_op jit(solution)/shard_map/all_to_all | solution.py:441
  10.5 0.6 %fusion.82 = f32[]{:T(128)} fusion(), kind=kLoop, calls=%fused_computation.210 | loop fusion | flops 3071 | bytes 4 | tf_op jit(solution)/shard_map/reduce_sum | solution.py:70
  11.2 1.9 %fusion.79.table_ref = bf16[512,512]{1,0:T(8,128)(2,1)} fusion(f32[]{:T(128)} %fusion.82, f32[512]{0:T(512)S(1)} %iota_convert_fusion), kind=kLoop, calls=%fused_computation.204 | loop fusion | flops 2359296 | bytes 526340 | tf_op jit(solution)/shard_map/convert_element_type | solution.py:71
  13.0 4.7 %ranks.1 = (f32[256,128]{1,0:T(8,128)}, s32[4,64,128]{2,1,0:T(8,128)S(1)}) custom-call(s32[1]{0:T(128)} %bitcast.10.slab_ref, s32[4,8192]{1,0:T(4,128)} %get-tuple-element.249.code_ref), custom_call_target="tpu_custom_call" | custom-call | tf_op jit(solution)/shard_map/ranks/pallas_call | solution.py:442
  17.7 0.0 all-to-all-done.6.msg_ref
  17.7 0.0 copy-start.1
  17.7 0.7 %copy-done.1 = bf16[16,32,128]{2,1,0:T(8,128)(2,1)} copy-done((bf16[16,32,128]{2,1,0:T(8,128)(2,1)}, bf16[16,32,128]{2,1,0:T(8,128)(2,1)S(1)}, u32[]{:S(2)}) %copy-start.1) | copy-done | bytes 131096
  18.4 10.1 %fields.1 = (bf16[4,4,1024]{2,1,0:T(4,128)(2,1)S(1)}, bf16[16,32,128]{2,1,0:T(8,128)(2,1)}) custom-call(s32[1]{0:T(128)} %bitcast.14.place_ref, bf16[16,32,128]{2,1,0:T(8,128)(2,1)} %copy-done.1, f32[256,128]{1,0:T(8,128)} %get-tuple-element.250.own_ref, bf16[512,512]{1,0:T(8,128)(2,1)} %fusion.79.table_ref), custom_call_target="tpu_custom_call" | custom-call | tf_op jit(solution)/shard_map/fields/pallas_call | solution.py:456
  28.5 10.7 %all-to-all-start.7 = ((bf16[16,32,128]{2,1,0:T(8,128)(2,1)}), bf16[16,32,128]{2,1,0:T(8,128)(2,1)S(1)}, u32[]{:S(2)}, u32[]{:S(2)}) async-start(bf16[16,32,128]{2,1,0:T(8,128)(2,1)} %get-tuple-element.251), calls=%async_computation.7 | async-start | bytes 262144 | tf_op jit(solution)/shard_map/all_to_all | solution.py:469
  39.2 1.4 %slice_reduce_fusion = bf16[]{:T(256)} fusion(bf16[16,32,128]{2,1,0:T(8,128)(2,1)} %copy-done.1), kind=kLoop, calls=%fused_computation.205 | loop fusion | flops 15 | bytes 34 | tf_op jit(solution)/shard_map/reduce_max | solution.py:470
  41.2 8.0 %all-to-all-done.7 = bf16[16,32,128]{2,1,0:T(8,128)(2,1)S(1)} async-done(((bf16[16,32,128]{2,1,0:T(8,128)(2,1)}), bf16[16,32,128]{2,1,0:T(8,128)(2,1)S(1)}, u32[]{:S(2)}, u32[]{:S(2)}) %all-to-all-start.7) | async-done | bytes 131104 | tf_op jit(solution)/shard_map/all_to_all | solution.py:469
  49.2 0.0 copy-done
  49.2 0.0 copy-done.2
  49.2 0.0 copy-done.3
  49.2 0.0 copy-done.4
  49.2 1.4 %conditional.1 = ((f32[2,8192]{1,0:T(2,128)S(1)}, bf16[4,4,1024]{2,1,0:T(4,128)(2,1)})) conditional(s32[]{:T(128)} %convert_element_type.68, (bf16[16,32,128]{2,1,0:T(8,128)(2,1)S(1)}, s32[4,64,128]{2,1,0:T(8,128)S(1)}, bf16[4,4,1024]{2,1,0:T(4,128)(2,1)S(1)}) %tuple.43, (s32[8192]{0:T(1024)S(1)}, s32[2,3,8192]{2,0,1:T(2,128)S(1)}, ...), branch_computations={%region_2.0_spmd, %region_3.15_spmd} | conditional | flops 1102073856 | bytes 41468728 | solution.py:484
  49.4 1.2 %changes.1 = (f32[2,8192]{1,0:T(2,128)S(1)}, bf16[4,4,1024]{2,1,0:T(4,128)(2,1)}) custom-call(bf16[16,32,128]{2,1,0:T(8,128)(2,1)S(1)} %get-tuple-element.217.value_ref, s32[4,64,128]{2,1,0:T(8,128)S(1)} %get-tuple-element.218.slot_ref, bf16[4,4,1024]{2,1,0:T(4,128)(2,1)S(1)} %get-tuple-element.219.field_in_ref), custom_call_target="tpu_custom_call" | custom-call | tf_op jit(solution)/shard_map/cond/branch_0_fun/changes/pallas_call | solution.py:473
  50.7 0.0 copy-start.6
  50.7 0.6 %copy-done.6 = f32[2,8192]{1,0:T(2,128)} copy-done((f32[2,8192]{1,0:T(2,128)}, f32[2,8192]{1,0:T(2,128)S(1)}, u32[]{:S(2)}) %copy-start.6) | copy-done | bytes 65560
  (1 shorter events, 0.0 us)
Async XLA Ops:
  4.9 44.4 %copy-start = (s32[2,3,8192]{2,0,1:T(2,128)S(1)}, s32[2,3,8192]{2,0,1:T(2,128)}, u32[]{:S(2)}) copy-start(s32[2,3,8192]{2,0,1:T(2,128)} %param.13) | copy-start | bytes 589828
  4.9 44.4 %copy-start.2 = (s32[8192]{0:T(1024)S(1)}, s32[8192]{0:T(1024)}, u32[]{:S(2)}) copy-start(s32[8192]{0:T(1024)} %param.12) | copy-start | bytes 98308
  4.9 44.4 %copy-start.3 = (s32[8192]{0:T(1024)S(1)}, s32[8192]{0:T(1024)}, u32[]{:S(2)}) copy-start(s32[8192]{0:T(1024)} %param.15) | copy-start | bytes 98308
  4.9 44.4 %copy-start.4 = (s32[2,8192]{1,0:T(2,128)S(1)}, s32[2,8192]{1,0:T(2,128)}, u32[]{:S(2)}) copy-start(s32[2,8192]{1,0:T(2,128)} %accepted_ref.1) | copy-start | bytes 196612
  4.9 12.9 %all-to-all-start.6 = ((bf16[16,32,128]{2,1,0:T(8,128)(2,1)}), bf16[16,32,128]{2,1,0:T(8,128)(2,1)S(1)}, u32[]{:S(2)}, u32[]{:S(2)}) async-start(bf16[16,32,128]{2,1,0:T(8,128)(2,1)} %get-tuple-element.248), calls=%async_computation.6 | async-start | bytes 262144 | tf_op jit(solution)/shard_map/all_to_all | solution.py:441
  17.7 0.7 %copy-start.1 = (bf16[16,32,128]{2,1,0:T(8,128)(2,1)}, bf16[16,32,128]{2,1,0:T(8,128)(2,1)S(1)}, u32[]{:S(2)}) copy-start(bf16[16,32,128]{2,1,0:T(8,128)(2,1)S(1)} %all-to-all-done.6.msg_ref) | copy-start | bytes 393220
  28.5 20.8 %all-to-all-start.7 = ((bf16[16,32,128]{2,1,0:T(8,128)(2,1)}), bf16[16,32,128]{2,1,0:T(8,128)(2,1)S(1)}, u32[]{:S(2)}, u32[]{:S(2)}) async-start(bf16[16,32,128]{2,1,0:T(8,128)(2,1)} %get-tuple-element.251), calls=%async_computation.7 | async-start | bytes 262144 | tf_op jit(solution)/shard_map/all_to_all | solution.py:469
  50.7 0.6 %copy-start.6 = (f32[2,8192]{1,0:T(2,128)}, f32[2,8192]{1,0:T(2,128)S(1)}, u32[]{:S(2)}) copy-start(f32[2,8192]{1,0:T(2,128)S(1)} %get-tuple-element.527) | copy-start | bytes 196612

commit v3 on v2

--- a/solution.py
+++ b/solution.py
@@ -13,8 +13,9 @@
 STEPS = 2
 SPREAD = 2
 SLABS = 16
-BANDS = 8
+BANDS = 16
 SLOTS = 128
+ROOMS = 64
 CHUNK = 256
 BLOCK = 1024
 SETS = 4
@@ -222,58 +223,65 @@
     code_ref[3:4, :] = second | kind
     c = code_ref[...]
     slabs[...] = ((c >> 17) & 15).astype(F32)
-    band = (c >> 12) & 7
+    band = (c >> 11) & 15
+    inside = ((c >> 17) & 15) == slab
     bands[0:SETS, :] = band.astype(F32)
-    bands[SETS : 2 * SETS, :] = jnp.where(((c >> 17) & 15) == slab, band, -64).astype(F32)
-    highs[...] = (((c >> 7) & 3) * 64 + (c >> 21) * 32 + ((c >> 9) & 7) * 4 + ((c >> 15) & 3) + 1).astype(F32)
+    bands[SETS : 2 * SETS, :] = jnp.where(inside, band, -64).astype(F32)
+    bands[2 * SETS : 3 * SETS, :] = jnp.where(inside, band & 7, -64).astype(F32)
+    bands[3 * SETS : 4 * SETS, :] = ((band >> 3) * ROOMS).astype(F32)
+    highs[...] = (((c >> 7) & 3) * 32 + (c >> 21) * 16 + ((c >> 9) & 3) * 4 + ((c >> 15) & 3) + 1).astype(F32)
     lows[...] = (c & 127).astype(F32)
-    counts = jnp.zeros((SETS * 16, 32), F32)
-    upper = lax.broadcasted_iota(jnp.int32, (16, CHUNK), 0) >= BANDS
-    own_row = (lax.broadcasted_iota(jnp.int32, (16, CHUNK), 0) & (BANDS - 1)).astype(F32).astype(BF16)
-    one = jnp.ones((16, CHUNK), BF16)
+    counts = jnp.zeros((SETS * 16, 48), F32)
+    upper = lax.broadcasted_iota(jnp.int32, (16, CHUNK), 0) >= 8
+    own_row = (lax.broadcasted_iota(jnp.int32, (16, CHUNK), 0) & 7).astype(F32).astype(BF16)
     zero = jnp.zeros((16, CHUNK), BF16)
-
-    def both(ref, base, lanes):
-        low = jnp.broadcast_to(ref[base : base + 1, lanes], (16, CHUNK))
-        high = jnp.broadcast_to(ref[base + 1 : base + 2, lanes], (16, CHUNK))
-        return jnp.where(upper, high, low).astype(BF16)
-
     for k in range(chunks):
         lanes = slice(k * CHUNK, (k + 1) * CHUNK)
         of_slab = jnp.concatenate([one_hot(slabs[s : s + 1, lanes], 16) for s in range(SETS)], axis=0)
-        of_band = jnp.where(both(bands, 0, lanes) == own_row, one, zero)
-        block = one_hot(jnp.full((1, CHUNK), float(k * CHUNK // BLOCK), F32), 16)
-        counts += lax.dot_general(of_slab, jnp.concatenate([of_band, block], axis=0), LANES, preferred_element_type=F32)
-        ranked[k * 16 : k * 16 + 16, :] = jnp.where(both(bands, SETS, lanes) == own_row, one, zero)
+        kinds = [one_hot(bands[s : s + 1, lanes], 16) for s in range(STEPS)]
+        kinds.append(one_hot(jnp.full((1, CHUNK), float(k * CHUNK // BLOCK), F32), 16))
+        counts += lax.dot_general(of_slab, jnp.concatenate(kinds, axis=0), LANES, preferred_element_type=F32)
+        for s in range(STEPS):
+            at = (s * chunks + k) * 16
+            ranked[at : at + 16, :] = one_hot(bands[SETS + s : SETS + s + 1, lanes], 16)
     set_of = lax.broadcasted_iota(jnp.int32, counts.shape, 0) // 16
-    column = lax.broadcasted_iota(jnp.int32, counts.shape, 1)
-    used = (column >= 16) | (set_of == column // BANDS)
-    crowded = jnp.max(jnp.where(used, counts, 0.0)) > float(SLOTS)
+    kind_of = lax.broadcasted_iota(jnp.int32, counts.shape, 1) // 16
+    limit = jnp.where(kind_of == STEPS, float(SLOTS), jnp.where(set_of == kind_of, float(ROOMS), float(beads)))
+    crowded = jnp.max(counts - limit) > 0.0
     prefix[...] = jnp.dot(ranked[...], prefix_matrix(), preferred_element_type=F32)
-    carry = jnp.zeros((16, 128), F32)
-    out = [jnp.zeros((16, SLOTS), F32), jnp.zeros((16, SLOTS), F32)]
-    for k in range(chunks):
-        lanes = slice(k * CHUNK, (k + 1) * CHUNK)
-        mine = ranked[k * 16 : k * 16 + 16, :]
-        ahead = mine.astype(F32) * (prefix[k * 16 : k * 16 + 16, 0:CHUNK] + jnp.concatenate([carry, carry], axis=1))
-        carry = carry + prefix[k * 16 : k * 16 + 16, CHUNK : CHUNK + 128]
-        for s in range(STEPS):
-            rank = jnp.sum(ahead[s * BANDS : (s + 1) * BANDS, :], axis=0, keepdims=True) - 1.0
+    out = []
+    for s in range(STEPS):
+        carry = jnp.zeros((16, 128), F32)
+        lists = jnp.zeros((16, SLOTS), F32)
+        for k in range(chunks):
+            at = (s * chunks + k) * 16
+            lanes = slice(k * CHUNK, (k + 1) * CHUNK)
+            ahead = prefix[at : at + 16, 0:CHUNK] + jnp.concatenate([carry, carry], axis=1)
+            carry = carry + prefix[at : at + 16, CHUNK : CHUNK + 128]
+            rank = jnp.sum(ranked[at : at + 16, :].astype(F32) * ahead, axis=0, keepdims=True) - 1.0
+            lane = jnp.where(rank >= 0.0, rank + bands[3 * SETS + s : 3 * SETS + s + 1, lanes], -1.0)
             low = jnp.broadcast_to(lows[s : s + 1, lanes], (16, CHUNK))
             high = jnp.broadcast_to(highs[s : s + 1, lanes], (16, CHUNK))
-            inside = jnp.broadcast_to(bands[SETS + s : SETS + s + 1, lanes], (16, CHUNK)).astype(BF16)
-            left = jnp.where(inside == own_row, jnp.where(upper, low, high).astype(BF16), zero)
-            out[s] += lax.dot_general(left, one_hot(rank, SLOTS), LANES, preferred_element_type=F32)
+            row = jnp.broadcast_to(bands[2 * SETS + s : 2 * SETS + s + 1, lanes], (16, CHUNK)).astype(BF16)
+            left = jnp.where(row == own_row, jnp.where(upper, low, high).astype(BF16), zero)
+            lists += lax.dot_general(left, one_hot(lane, SLOTS), LANES, preferred_element_type=F32)
+        out.append(lists)
     corner = (lax.broadcasted_iota(jnp.int32, (16, SLOTS), 0) == 0) & (
         lax.broadcasted_iota(jnp.int32, (16, SLOTS), 1) == 0
     )
     out[0] = jnp.where(corner & crowded, MARK, out[0])
-    lists = jnp.concatenate(out, axis=0).astype(BF16)
+    message = jnp.concatenate(out, axis=0).astype(BF16)
     for j in range(SLABS):
-        msg_ref[j] = lists
-
-
-def rank_kernel(slab_ref, code_ref, own_ref, slot_ref, slabs, digits, ranked, prefix):
+        msg_ref[j] = message
+
+
+def rank_kernel(scale, slab_ref, code_ref, own_ref, slot_ref, table_ref, slabs, digits, ranked, prefix):
+    column = lax.broadcasted_iota(jnp.int32, (8, NX), 1)
+    distance = jnp.minimum(column, NX - column).astype(F32)
+    weights = jnp.exp(-distance * distance / (2.0 * SPREAD * SPREAD))
+    first = (weights / jnp.sum(weights[0:1, :], axis=1, keepdims=True))[0:1, :]
+    turned = pltpu.roll(jnp.broadcast_to(first, (NX, NX)), 0, 1, stride=1, stride_axis=0)
+    table_ref[...] = turned.astype(BF16) * jnp.full((NX, NX), scale, BF16)
     beads = code_ref.shape[1]
     chunks = beads // CHUNK
     c = code_ref[...]
@@ -309,55 +317,93 @@
             own_ref[at : at + 8, :] = lists[0:8, :]
 
 
-def field_kernel(scale, place_ref, msg_ref, own_ref, table_ref, field_ref, value_ref,
-                 count_lo, count_hi, field, values):
+def field_kernel(place_ref, msg_ref, own_ref, table_ref, field_ref, value_ref, crowd_ref,
+                 slots, count, count_lo, count_hi, dens, field, values):
     blocks = own_ref.shape[0] // (8 * SETS)
     half = ROWS * 2
+    marks = msg_ref[0, 0:1, :].astype(F32)
+    for j in range(1, SLABS):
+        marks = jnp.maximum(marks, msg_ref[j, 0:1, :].astype(F32))
+    crowd_ref[0] = (jnp.max(marks) >= MARK).astype(jnp.int32)
+    most = jnp.zeros((8, SLOTS), F32)
+    left_half = lax.broadcasted_iota(jnp.int32, (32, SLOTS), 1) < ROOMS
+    for j in range(0, SLABS, 2):
+        even, odd = msg_ref[j].astype(F32), msg_ref[j + 1].astype(F32)
+        lanes = slice(j // 2 * SLOTS, (j // 2 + 1) * SLOTS)
+        slots[0, :, lanes] = jnp.where(left_half, even, pltpu.roll(odd, ROOMS, 1))
+        slots[1, :, lanes] = jnp.where(left_half, pltpu.roll(even, ROOMS, 1), odd)
     for step in range(STEPS):
         for band in range(BANDS):
-            hist = jnp.zeros((256, SLOTS), F32)
-            for j in range(0, SLABS, 2):
-                at = step * 16 + band
-                high = [msg_ref[i, at : at + 1, :].astype(F32) for i in (j, j + 1)]
-                low = [msg_ref[i, at + BANDS : at + BANDS + 1, :].astype(F32) for i in (j, j + 1)]
+            hist = jnp.zeros((128, 128), F32)
+            at = step * 16 + band % 8
+            for k in range(0, slots.shape[2], CHUNK):
                 hist += lax.dot_general(
-                    one_hot(jnp.concatenate(high, axis=1), 256, 1),
-                    one_hot(jnp.concatenate(low, axis=1), 128),
+                    one_hot(slots[band // 8, at : at + 1, k : k + CHUNK], 128, 1),
+                    one_hot(slots[band // 8, at + 8 : at + 9, k : k + CHUNK], 128),
                     LANES,
                     preferred_element_type=F32,
                 )
-            upper = jnp.floor(hist * (1.0 / 256.0))
-            lower = hist - 256.0 * upper
             for q in range(4):
                 for t in range(2):
-                    at = step * half + t * ROWS + band * 32
-                    rows = slice(q * 64 + t * 32, q * 64 + t * 32 + 32)
-                    count_lo[at : at + 32, q * 128 : (q + 1) * 128] = lower[rows, :].astype(BF16)
-                    count_hi[at : at + 32, q * 128 : (q + 1) * 128] = upper[rows, :].astype(BF16)
+                    at = step * half + t * ROWS + band * 16
+                    part = hist[q * 32 + t * 16 : q * 32 + t * 16 + 16, :]
+                    count[at : at + 16, q * 128 : (q + 1) * 128] = part
+                    count_lo[at : at + 16, q * 128 : (q + 1) * 128] = part.astype(BF16)
+                    most = jnp.maximum(most, jnp.maximum(part[0:8, :], part[8:16, :]))
+    many = jnp.max(most) > 256.0
 
     def mixed(phi_a, phi_b):
         excess = kappa_comp * (phi_a + phi_b - 1.0)
         return (chi_mix * phi_b + excess).astype(BF16), (chi_mix * phi_a + excess).astype(BF16)
 
-    table = table_ref[...]
-    for step in range(STEPS):
-        rows = slice(step * half, (step + 1) * half)
-        dens = lax.dot_general(table, count_lo[rows, :], LANES, preferred_element_type=F32)
-        dens += 256.0 * lax.dot_general(table, count_hi[rows, :], LANES, preferred_element_type=F32)
-        dens = dens * scale
-        field_a, field_b = mixed(dens[:, 0:ROWS], dens[:, ROWS:])
-        field[step, :, 0:ROWS] = field_a
-        field[step, :, ROWS:] = field_b
-    at = (STEPS - 1) * half + place_ref[0] * 16
-    mine = []
-    for t in range(2):
-        rows = pl.ds(pl.multiple_of(at + t * ROWS, 16), 16)
-        dens = jnp.dot(count_lo[rows, :], table, preferred_element_type=F32)
-        dens += 256.0 * jnp.dot(count_hi[rows, :], table, preferred_element_type=F32)
-        mine.append(dens * scale)
-    for t, part in enumerate(mixed(*mine)):
-        for y in range(4):
-            field_ref[y, :, t * NX : (t + 1) * NX] = part[y * ZDEV : (y + 1) * ZDEV, :]
+    def whole(counts):
+        return [
+            lax.dot_general(table_ref[...], counts[step * half : (step + 1) * half, :], LANES, preferred_element_type=F32)
+            for step in range(STEPS)
+        ]
+
+    def own(digit):
+        at = (STEPS - 1) * half + place_ref[0] * 16
+        return [
+            jnp.dot(
+                digit(count[pl.ds(pl.multiple_of(at + t * ROWS, 16), 16), :]).astype(BF16),
+                table_ref[...],
+                preferred_element_type=F32,
+            )
+            for t in range(2)
+        ]
+
+    def store_fields(dens, mine):
+        for step in range(STEPS):
+            field_a, field_b = mixed(dens[step][:, 0:ROWS], dens[step][:, ROWS:])
+            field[step, :, 0:ROWS] = field_a
+            field[step, :, ROWS:] = field_b
+        for t, part in enumerate(mixed(*mine)):
+            for y in range(4):
+                field_ref[y, :, t * NX : (t + 1) * NX] = part[y * ZDEV : (y + 1) * ZDEV, :]
+
+    def upper(rows):
+        return jnp.floor(rows * (1.0 / 256.0))
+
+    def lower(rows):
+        return rows - 256.0 * upper(rows)
+
+    @pl.when(jnp.logical_not(many))
+    def _():
+        store_fields(whole(count_lo), own(lambda rows: rows))
+
+    @pl.when(many)
+    def _():
+        for i in range(0, STEPS * half, 64):
+            count_lo[i : i + 64, :] = lower(count[i : i + 64, :]).astype(BF16)
+            count_hi[i : i + 64, :] = upper(count[i : i + 64, :]).astype(BF16)
+        for step, part in enumerate(whole(count_hi)):
+            dens[step] = 256.0 * part
+        store_fields(
+            [dens[step] + part for step, part in enumerate(whole(count_lo))],
+            [256.0 * a + b for a, b in zip(own(upper), own(lower))],
+        )
+
     column = lax.broadcasted_iota(jnp.int32, (256, CHUNK), 0).astype(F32)
     for step in range(STEPS):
         for which in range(2):
@@ -385,7 +431,9 @@
         value_ref[j] = lists
 
 
-def change_kernel(value_ref, slot_ref, field_in_ref, change_ref, field_ref):
+def change_kernel(value_ref, slot_ref, field_in_ref, change_out, field_out, change_ref, sems):
+    field_copy = pltpu.make_async_copy(field_in_ref, field_out, sems.at[0])
+    field_copy.start()
     lines = slot_ref.shape[1]
     blocks = lines * 128 // BLOCK
     for step in range(STEPS):
@@ -405,11 +453,16 @@
             for i in range(8):
                 lanes = slice((block * 8 + i) * 128, (block * 8 + i + 1) * 128)
                 change_ref[step : step + 1, lanes] = change[i : i + 1, :]
-    field_ref[...] = field_in_ref[...]
+    change_copy = pltpu.make_async_copy(change_ref, change_out, sems.at[1])
+    change_copy.start()
+    field_copy.wait()
+    change_copy.wait()
 
 
 VMEM = pl.BlockSpec(memory_space=pltpu.VMEM)
 SMEM = pl.BlockSpec(memory_space=pltpu.SMEM)
+HBM = pl.BlockSpec(memory_space=pltpu.HBM)
+ROOM = pltpu.CompilerParams(vmem_limit_bytes=24 * 2**20)
 
 
 def shape(dims, dtype):
@@ -428,22 +481,28 @@
         out_shape=(shape((SLABS, 32, SLOTS), BF16), shape((SETS, beads), jnp.int32)),
         in_specs=[SMEM] + [VMEM] * 4,
         out_specs=(VMEM, VMEM),
+        compiler_params=ROOM,
         scratch_shapes=[
             pltpu.VMEM((SETS, beads), F32),
-            pltpu.VMEM((2 * SETS, beads), F32),
+            pltpu.VMEM((4 * SETS, beads), F32),
             pltpu.VMEM((SETS, beads), F32),
             pltpu.VMEM((SETS, beads), F32),
-            pltpu.VMEM((chunks * 16, CHUNK), BF16),
-            pltpu.VMEM((chunks * 16, CHUNK + 128), F32),
+            pltpu.VMEM((STEPS * chunks * 16, CHUNK), BF16),
+            pltpu.VMEM((STEPS * chunks * 16, CHUNK + 128), F32),
         ],
         name="bucket",
     )(slab, cells_start.reshape(1, beads), jnp.moveaxis(moves, 1, 0), accepted, bead_types.reshape(1, beads))
     msg = lax.all_to_all(msg, "mol", split_axis=0, concat_axis=0, tiled=True)
-    own, slot = pl.pallas_call(
-        rank_kernel,
-        out_shape=(shape((SETS * blocks * 8, SLOTS), F32), shape((SETS, beads // 128, 128), jnp.int32)),
+    own, slot, table = pl.pallas_call(
+        functools.partial(rank_kernel, scale),
+        out_shape=(
+            shape((SETS * blocks * 8, SLOTS), F32),
+            shape((SETS, beads // 128, 128), jnp.int32),
+            shape((NX, NX), BF16),
+        ),
         in_specs=[SMEM, VMEM],
-        out_specs=(VMEM, VMEM),
+        out_specs=(VMEM, VMEM, VMEM),
+        compiler_params=ROOM,
         scratch_shapes=[
             pltpu.VMEM((SETS, beads), F32),
             pltpu.VMEM((3 * SETS, beads), F32),
@@ -452,36 +511,44 @@
         ],
         name="ranks",
     )(slab, code)
-    table = kernel_rows(jnp.arange(NX, dtype=jnp.int32))
-    field, value = pl.pallas_call(
-        functools.partial(field_kernel, scale),
-        out_shape=(shape((4, ZDEV, 2 * NX), BF16), shape((SLABS, SETS * blocks, SLOTS), BF16)),
+    field, value, crowd = pl.pallas_call(
+        field_kernel,
+        out_shape=(
+            shape((4, ZDEV, 2 * NX), BF16),
+            shape((SLABS, SETS * blocks, SLOTS), BF16),
+            shape((1,), jnp.int32),
+        ),
         in_specs=[SMEM] + [VMEM] * 3,
-        out_specs=(VMEM, VMEM),
+        out_specs=(VMEM, VMEM, SMEM),
+        compiler_params=ROOM,
         scratch_shapes=[
+            pltpu.VMEM((2, 32, SLABS * ROOMS), F32),
+            pltpu.VMEM((STEPS * ROWS * 2, NX), F32),
             pltpu.VMEM((STEPS * ROWS * 2, NX), BF16),
             pltpu.VMEM((STEPS * ROWS * 2, NX), BF16),
+            pltpu.VMEM((STEPS, NX, ROWS * 2), F32),
             pltpu.VMEM((STEPS, NX, ROWS * 2), BF16),
             pltpu.VMEM((SETS * blocks, SLOTS), F32),
         ],
         name="fields",
     )(place, msg, own, table)
     value = lax.all_to_all(value, "grid", split_axis=0, concat_axis=0, tiled=True)
-    crowded = jnp.max(msg[:, 0, 0].astype(F32)) >= MARK
 
     def bucketed(value, slot, field, *_):
         return pl.pallas_call(
             change_kernel,
             out_shape=(shape((STEPS, beads), F32), shape(field.shape, BF16)),
             in_specs=[VMEM] * 3,
-            out_specs=(VMEM, VMEM),
+            out_specs=(HBM, HBM),
+            scratch_shapes=[pltpu.VMEM((STEPS, beads), F32), pltpu.SemaphoreType.DMA((2,))],
+            compiler_params=ROOM,
             name="changes",
         )(value, slot, field)
 
     def general(value, slot, field, *arguments):
         return any_spread(*arguments)
 
-    return lax.cond(crowded, general, bucketed, value, slot, field, cells_start, moves, accepted, bead_types)
+    return lax.cond(crowd[0] == 1, general, bucketed, value, slot, field, cells_start, moves, accepted, bead_types)
 
 
 def solution(mesh):

time: 52.3 us -> 45.3 us (0.87); the launches traced: 51.3 us -> 45 us
  Pallas kernels: 20.2 us -> 14.1 us
  waiting for transfers between devices: 7.98 us -> 12.4 us
  other arithmetic: 3.87 us -> 0 us
  local copies, waits for them, and re-layouts: 1.31 us -> 0.64 us
    pallas_call x2, Pallas kernels: 14.8 us -> 9.66 us  [the longest x1 6.48 us: local(): pl.pallas_call(field_kernel, out_shape=(shape((4, ZDEV, 2 * NX), BF16), s...]
    all_to_all x1, waiting for transfers between devices: 0.01 us -> 3.47 us  [local(): msg = lax.all_to_all(msg, 'mol', split_axis=0, concat_axis=0, tiled=True)]
    convert_element_type x2 -> x0, other arithmetic: 1.87 us -> none  [the longest x1 1.87 us: kernel_rows(): return (weights / total).astype(jnp.bfloat16)]
    reduce_max x1 -> x0, other arithmetic: 1.38 us -> none  [local(): crowded = jnp.max(msg[:, 0, 0].astype(F32)) >= MARK]
    all_to_all x1, waiting for transfers between devices: 7.97 us -> 8.94 us  [local(): lax.all_to_all(value, 'grid', split_axis=0, concat_axis=0, tiled=True)]
    unnamed x12 -> x10, local copies, waits for them, and re-layouts: 1.31 us -> 0.64 us
    reduce_sum x1 -> x0, other arithmetic: 0.62 us -> none  [kernel_rows(): total = jnp.sum(jnp.exp(-first * first / (2.0 * SPREAD * SPREAD)))]
    pallas_call x1, Pallas kernels: 4.23 us -> 3.62 us  [local(): pl.pallas_call(bucket_kernel, out_shape=(shape((SLABS, 32, SLOTS), BF16),...]
  transfers between devices with their start and end apart: 2 -> 2, of which waited for: 1 -> 2; matrix products, arithmetic and copies ran while one was open for 8% -> 0% of each run, Pallas kernels for 9% -> 7%
where the time goes in v3:
time: 45.3 us; the launch traced here: 45 us
  starting transfers between devices  16.3 us (36%)
  Pallas kernels  14.1 us (31%)
  waiting for transfers between devices  12.4 us (27%)
  between operations  1.38 us (3%)
  local copies, waits for them, and re-layouts  0.64 us (1%)
    all_to_all x1, starting transfers between devices, local(): lax.all_to_all(value, 'grid', split_axis=0, concat_axis=0, tiled=True)  10.8 us
    all_to_all x1, waiting for transfers between devices, local(): lax.all_to_all(value, 'grid', split_axis=0, concat_axis=0, tiled=True)  8.94 us
    pallas_call x1, Pallas kernels, local(): pl.pallas_call(field_kernel, out_shape=(shape((4, ZDEV, 2 * NX), BF16), s...  6.48 us
    all_to_all x1, starting transfers between devices, local(): msg = lax.all_to_all(msg, 'mol', split_axis=0, concat_axis=0, tiled=True)  5.5 us
    pallas_call x1, Pallas kernels, local(): pl.pallas_call(bucket_kernel, out_shape=(shape((SLABS, 32, SLOTS), BF16),...  3.62 us
    all_to_all x1, waiting for transfers between devices, local(): msg = lax.all_to_all(msg, 'mol', split_axis=0, concat_axis=0, tiled=True)  3.47 us
    pallas_call x1, Pallas kernels, local(): pl.pallas_call(functools.partial(rank_kernel, scale), out_shape=(shape((S...  3.19 us
  transfers between devices with their start and end apart: 2, of which 2 were waited for; matrix products, arithmetic and copies ran while one was open for 0% of the time, Pallas kernels for 7%

profile of v3, /device:TPU:32, one launch (start us, length us, event | category | flops | bytes accessed | tf_op | source)
XLA Modules:
  0.0 45.0 jit_solution(3202574002153817649)
XLA Ops:
  0.6 0.0 copy-start.1
  0.6 0.0 copy-start
  0.7 0.0 copy-start.3
  0.7 0.0 copy-start.2
  0.7 3.6 %bucket.1 = (bf16[16,32,128]{2,1,0:T(8,128)(2,1)}, s32[4,8192]{1,0:T(4,128)S(1)}) custom-call(s32[1]{0:T(128)} %bitcast.11.slab_ref, s32[1,8192]{1,0:T(1,128)} %bitcast.31, s32[3,2,8192]{2,1,0:T(2,128)} %bitcast.28, s32[2,8192]{1,0:T(2,128)} %accepted_ref.1, s32[1,8192]{1,0:T(1,128)} %bitcast.36), custom_call_target="tpu_custom_call" | custom-call | tf_op jit(solution)/shard_map/bucket/pallas_call | solution.py:479
  4.3 5.5 %all-to-all-start.6 = ((bf16[16,32,128]{2,1,0:T(8,128)(2,1)}), bf16[16,32,128]{2,1,0:T(8,128)(2,1)S(1)}, u32[]{:S(2)}, u32[]{:S(2)}) async-start(bf16[16,32,128]{2,1,0:T(8,128)(2,1)} %get-tuple-element.250), calls=%async_computation.6 | async-start | bytes 262144 | tf_op jit(solution)/shard_map/all_to_all | solution.py:495
  9.8 3.2 %ranks.1 = (f32[256,128]{1,0:T(8,128)S(1)}, s32[4,64,128]{2,1,0:T(8,128)S(1)}, bf16[512,512]{1,0:T(8,128)(2,1)S(1)}) custom-call(s32[1]{0:T(128)} %bitcast.11.slab_ref, s32[4,8192]{1,0:T(4,128)S(1)} %get-tuple-element.251.code_ref), custom_call_target="tpu_custom_call" | custom-call | tf_op jit(solution)/shard_map/ranks/pallas_call | solution.py:496
  13.0 3.5 %all-to-all-done.6.msg_ref = bf16[16,32,128]{2,1,0:T(8,128)(2,1)S(1)} async-done(((bf16[16,32,128]{2,1,0:T(8,128)(2,1)}), bf16[16,32,128]{2,1,0:T(8,128)(2,1)S(1)}, u32[]{:S(2)}, u32[]{:S(2)}) %all-to-all-start.6) | async-done | bytes 131104 | tf_op jit(solution)/shard_map/all_to_all | solution.py:495
  16.5 6.5 %fields.1 = (bf16[4,4,1024]{2,1,0:T(4,128)(2,1)S(1)}, bf16[16,32,128]{2,1,0:T(8,128)(2,1)}, s32[1]{0:T(128)}) custom-call(s32[1]{0:T(128)} %bitcast.10.place_ref, bf16[16,32,128]{2,1,0:T(8,128)(2,1)S(1)} %all-to-all-done.6.msg_ref, f32[256,128]{1,0:T(8,128)S(1)} %get-tuple-element.252.own_ref, bf16[512,512]{1,0:T(8,128)(2,1)S(1)} %get-tuple-element.253.table_ref), custom_call_target="tpu_custom_call" | custom-call | tf_op jit(solution)/shard_map/fields/pallas_call | solution.py:514
  23.0 10.8 %all-to-all-start.7 = ((bf16[16,32,128]{2,1,0:T(8,128)(2,1)}), bf16[16,32,128]{2,1,0:T(8,128)(2,1)S(1)}, u32[]{:S(2)}, u32[]{:S(2)}) async-start(bf16[16,32,128]{2,1,0:T(8,128)(2,1)} %get-tuple-element.255), calls=%async_computation.7 | async-start | bytes 262144 | tf_op jit(solution)/shard_map/all_to_all | solution.py:535
  34.4 8.9 %all-to-all-done.7 = bf16[16,32,128]{2,1,0:T(8,128)(2,1)S(1)} async-done(((bf16[16,32,128]{2,1,0:T(8,128)(2,1)}), bf16[16,32,128]{2,1,0:T(8,128)(2,1)S(1)}, u32[]{:S(2)}, u32[]{:S(2)}) %all-to-all-start.7) | async-done | bytes 131104 | tf_op jit(solution)/shard_map/all_to_all | solution.py:535
  43.3 0.0 copy-done.1
  43.3 0.0 copy-done
  43.3 0.0 copy-done.3
  43.3 0.0 copy-done.2
  43.3 1.1 %conditional.1 = ((f32[2,8192]{1,0:T(2,128)S(1)}, bf16[4,4,1024]{2,1,0:T(4,128)(2,1)})) conditional(s32[]{:T(128)} %bitcast.15, (bf16[16,32,128]{2,1,0:T(8,128)(2,1)S(1)}, s32[4,64,128]{2,1,0:T(8,128)S(1)}, bf16[4,4,1024]{2,1,0:T(4,128)(2,1)S(1)}) %tuple.43, (s32[8192]{0:T(1024)S(1)}, s32[2,3,8192]{2,0,1:T(2,128)S(1)}, s32[8192]{0:T(1024)S(1)}, ...), branch_computations={%region_0.0_spmd, %region_1.13_spmd} | conditional | flops 1102073856 | bytes 41468728 | solution.py:551
  43.4 0.8 %changes.1 = (f32[2,8192]{1,0:T(2,128)S(1)}, bf16[4,4,1024]{2,1,0:T(4,128)(2,1)}) custom-call(bf16[16,32,128]{2,1,0:T(8,128)(2,1)S(1)} %get-tuple-element.217.value_ref, s32[4,64,128]{2,1,0:T(8,128)S(1)} %get-tuple-element.218.slot_ref, bf16[4,4,1024]{2,1,0:T(4,128)(2,1)S(1)} %get-tuple-element.219.field_in_ref), custom_call_target="tpu_custom_call" | custom-call | tf_op jit(solution)/shard_map/cond/branch_0_fun/changes/pallas_call | solution.py:538
  44.4 0.0 copy-start.5
  44.4 0.6 %copy-done.5 = f32[2,8192]{1,0:T(2,128)} copy-done((f32[2,8192]{1,0:T(2,128)}, f32[2,8192]{1,0:T(2,128)S(1)}, u32[]{:S(2)}) %copy-start.5) | copy-done | bytes 65560
Async XLA Ops:
  0.6 42.7 %copy-start.1 = (s32[8192]{0:T(1024)S(1)}, s32[8192]{0:T(1024)}, u32[]{:S(2)}) copy-start(s32[8192]{0:T(1024)} %param.12) | copy-start | bytes 98308
  0.6 42.7 %copy-start = (s32[2,3,8192]{2,0,1:T(2,128)S(1)}, s32[2,3,8192]{2,0,1:T(2,128)}, u32[]{:S(2)}) copy-start(s32[2,3,8192]{2,0,1:T(2,128)} %param.13) | copy-start | bytes 589828
  0.7 42.7 %copy-start.3 = (s32[2,8192]{1,0:T(2,128)S(1)}, s32[2,8192]{1,0:T(2,128)}, u32[]{:S(2)}) copy-start(s32[2,8192]{1,0:T(2,128)} %accepted_ref.1) | copy-start | bytes 196612
  0.7 42.7 %copy-start.2 = (s32[8192]{0:T(1024)S(1)}, s32[8192]{0:T(1024)}, u32[]{:S(2)}) copy-start(s32[8192]{0:T(1024)} %param.15) | copy-start | bytes 98308
  4.3 12.2 %all-to-all-start.6 = ((bf16[16,32,128]{2,1,0:T(8,128)(2,1)}), bf16[16,32,128]{2,1,0:T(8,128)(2,1)S(1)}, u32[]{:S(2)}, u32[]{:S(2)}) async-start(bf16[16,32,128]{2,1,0:T(8,128)(2,1)} %get-tuple-element.250), calls=%async_computation.6 | async-start | bytes 262144 | tf_op jit(solution)/shard_map/all_to_all | solution.py:495
  23.0 20.4 %all-to-all-start.7 = ((bf16[16,32,128]{2,1,0:T(8,128)(2,1)}), bf16[16,32,128]{2,1,0:T(8,128)(2,1)S(1)}, u32[]{:S(2)}, u32[]{:S(2)}) async-start(bf16[16,32,128]{2,1,0:T(8,128)(2,1)} %get-tuple-element.255), calls=%async_computation.7 | async-start | bytes 262144 | tf_op jit(solution)/shard_map/all_to_all | solution.py:535
  44.4 0.6 %copy-start.5 = (f32[2,8192]{1,0:T(2,128)}, f32[2,8192]{1,0:T(2,128)S(1)}, u32[]{:S(2)}) copy-start(f32[2,8192]{1,0:T(2,128)S(1)} %get-tuple-element.527) | copy-start | bytes 196612

commit v4 on v3

--- a/solution.py
+++ b/solution.py
@@ -190,14 +190,6 @@
     rows = lax.broadcasted_iota(jnp.int32, (CHUNK, CHUNK + 128), 0)
     cols = lax.broadcasted_iota(jnp.int32, (CHUNK, CHUNK + 128), 1)
     return jnp.where((rows <= cols) | (cols >= CHUNK), 1.0, 0.0).astype(BF16)
-
-
-def stacked(rows, width):
-    iota = lax.broadcasted_iota(jnp.int32, (16, width), 0)
-    total = jnp.zeros((16, width), F32)
-    for i, row in enumerate(rows):
-        total = jnp.where(iota == i, jnp.broadcast_to(row, (16, width)), total)
-    return total.astype(BF16)
 
 
 def bucket_kernel(slab_ref, cells_ref, moves_ref, accepted_ref, types_ref, msg_ref, code_ref,
@@ -237,7 +229,9 @@
     zero = jnp.zeros((16, CHUNK), BF16)
     for k in range(chunks):
         lanes = slice(k * CHUNK, (k + 1) * CHUNK)
-        of_slab = jnp.concatenate([one_hot(slabs[s : s + 1, lanes], 16) for s in range(SETS)], axis=0)
+        alone = [one_hot(slabs[s : s + 1, lanes], 16) for s in range(SETS)]
+        either = [jnp.maximum(alone[s], alone[STEPS + s]) for s in range(STEPS)]
+        of_slab = jnp.concatenate(alone[0:STEPS] + either, axis=0)
         kinds = [one_hot(bands[s : s + 1, lanes], 16) for s in range(STEPS)]
         kinds.append(one_hot(jnp.full((1, CHUNK), float(k * CHUNK // BLOCK), F32), 16))
         counts += lax.dot_general(of_slab, jnp.concatenate(kinds, axis=0), LANES, preferred_element_type=F32)
@@ -246,7 +240,8 @@
             ranked[at : at + 16, :] = one_hot(bands[SETS + s : SETS + s + 1, lanes], 16)
     set_of = lax.broadcasted_iota(jnp.int32, counts.shape, 0) // 16
     kind_of = lax.broadcasted_iota(jnp.int32, counts.shape, 1) // 16
-    limit = jnp.where(kind_of == STEPS, float(SLOTS), jnp.where(set_of == kind_of, float(ROOMS), float(beads)))
+    listed = (kind_of == STEPS) & (set_of >= STEPS)
+    limit = jnp.where(listed, float(SLOTS), jnp.where(set_of == kind_of, float(ROOMS), float(beads)))
     crowded = jnp.max(counts - limit) > 0.0
     prefix[...] = jnp.dot(ranked[...], prefix_matrix(), preferred_element_type=F32)
     out = []
@@ -285,41 +280,56 @@
     beads = code_ref.shape[1]
     chunks = beads // CHUNK
     c = code_ref[...]
-    slabs[...] = ((c >> 17) & 15).astype(F32)
+    home = (c >> 17) & 15
+    slabs[...] = home.astype(F32)
     digits[0:SETS, :] = (((c >> 9) & 63) * 4 + ((c >> 15) & 3)).astype(F32)
-    digits[SETS : 2 * SETS, :] = ((c >> 21) * 2 + ((c >> 8) & 1) + 1).astype(F32)
+    digits[SETS : 2 * SETS, :] = jnp.where(home == slab_ref[0], (c >> 21) * 2 + ((c >> 8) & 1) + 1, 0).astype(F32)
     digits[2 * SETS : 3 * SETS, :] = (c & 255).astype(F32)
     here = slab_ref[0].astype(F32)
-    for s in range(SETS):
+    for s in range(STEPS):
         for k in range(chunks):
             at = (s * chunks + k) * 16
-            ranked[at : at + 16, :] = one_hot(slabs[s : s + 1, k * CHUNK : (k + 1) * CHUNK], 16)
+            lanes = slice(k * CHUNK, (k + 1) * CHUNK)
+            ranked[at : at + 16, :] = jnp.maximum(
+                one_hot(slabs[s : s + 1, lanes], 16), one_hot(slabs[STEPS + s : STEPS + s + 1, lanes], 16)
+            )
     prefix[...] = jnp.dot(ranked[...], prefix_matrix(), preferred_element_type=F32)
-    for s in range(SETS):
+    sixteen = lax.broadcasted_iota(jnp.int32, (16, CHUNK), 0).astype(F32)
+    eight = lax.broadcasted_iota(jnp.int32, (8, CHUNK), 0)
+    for s in range(STEPS):
         for block in range(beads // BLOCK):
             carry = jnp.zeros((16, 128), F32)
-            lists = jnp.zeros((16, SLOTS), F32)
+            lists = jnp.zeros((8, SLOTS), F32)
             for k in range(block * BLOCK // CHUNK, (block + 1) * BLOCK // CHUNK):
                 at = (s * chunks + k) * 16
                 lanes = slice(k * CHUNK, (k + 1) * CHUNK)
                 ahead = prefix[at : at + 16, 0:CHUNK] + jnp.concatenate([carry, carry], axis=1)
                 carry = carry + prefix[at : at + 16, CHUNK : CHUNK + 128]
-                rank = jnp.sum(ranked[at : at + 16, :].astype(F32) * ahead, axis=0, keepdims=True) - 1.0
-                home = slabs[s : s + 1, lanes]
-                slot = (home * float(SLOTS) + rank).astype(jnp.int32)
-                for i in range(CHUNK // 128):
-                    line = k * CHUNK // 128 + i
-                    slot_ref[s, line : line + 1, :] = slot[:, i * 128 : (i + 1) * 128]
-                held = jnp.where(home == here, rank, -1.0)
-                left = stacked([digits[d * SETS + s : d * SETS + s + 1, lanes] for d in range(3)], CHUNK)
-                lists += lax.dot_general(left, one_hot(held, SLOTS), LANES, preferred_element_type=F32)
+                homes, ranks = [], []
+                for p in (s, STEPS + s):
+                    homes.append(slabs[p : p + 1, lanes])
+                    mine = jnp.where(sixteen == jnp.broadcast_to(homes[-1], (16, CHUNK)), ahead, 0.0)
+                    ranks.append(jnp.sum(mine, axis=0, keepdims=True) - 1.0)
+                first = homes[0] * float(SLOTS) + ranks[0]
+                second = jnp.where(homes[0] == homes[1], float(-SLOTS), homes[1] * float(SLOTS) + ranks[1])
+                for p, slot in ((s, first.astype(jnp.int32)), (STEPS + s, second.astype(jnp.int32))):
+                    for i in range(CHUNK // 128):
+                        line = k * CHUNK // 128 + i
+                        slot_ref[p, line : line + 1, :] = slot[:, i * 128 : (i + 1) * 128]
+                held = jnp.where(homes[0] == here, ranks[0], jnp.where(homes[1] == here, ranks[1], -1.0))
+                left = jnp.zeros((8, CHUNK), F32)
+                for d in range(6):
+                    row = d % 3 * SETS + d // 3 * STEPS + s
+                    left = jnp.where(eight == d, jnp.broadcast_to(digits[row : row + 1, lanes], (8, CHUNK)), left)
+                lists += lax.dot_general(left.astype(BF16), one_hot(held, SLOTS), LANES, preferred_element_type=F32)
             at = (s * (beads // BLOCK) + block) * 8
-            own_ref[at : at + 8, :] = lists[0:8, :]
+            own_ref[at : at + 8, :] = lists
+    own_ref[STEPS * chunks * CHUNK // 128 :, :] = jnp.zeros((8, SLOTS), F32)
 
 
 def field_kernel(place_ref, msg_ref, own_ref, table_ref, field_ref, value_ref, crowd_ref,
                  slots, count, count_lo, count_hi, dens, field, values):
-    blocks = own_ref.shape[0] // (8 * SETS)
+    blocks = (own_ref.shape[0] - 8) // (8 * STEPS)
     half = ROWS * 2
     marks = msg_ref[0, 0:1, :].astype(F32)
     for j in range(1, SLABS):
@@ -406,14 +416,14 @@
 
     column = lax.broadcasted_iota(jnp.int32, (256, CHUNK), 0).astype(F32)
     for step in range(STEPS):
-        for which in range(2):
-            for block in range(0, blocks, 2):
-                at = ((which * STEPS + step) * blocks + block) * 8
-
-                def digit(d):
-                    return jnp.concatenate([own_ref[at + d : at + d + 1, :], own_ref[at + 8 + d : at + 9 + d, :]], axis=1)
-
-                row, part, low = digit(0), digit(1), digit(2)
+        for block in range(0, blocks, 2):
+            at = (step * blocks + block) * 8
+            read = []
+            for which in range(2):
+                row, part, low = [
+                    jnp.concatenate([own_ref[at + d : at + d + 1, :], own_ref[at + 8 + d : at + 9 + d, :]], axis=1)
+                    for d in range(which * 3, which * 3 + 3)
+                ]
                 picked = jnp.zeros((256, CHUNK), F32)
                 for q in range(4):
                     x_at, t_at = (q & 1) * 256, (q >> 1) * ROWS
@@ -422,46 +432,42 @@
                         one_hot(jnp.where(part == q + 1.0, row, -1.0), ROWS),
                         preferred_element_type=F32,
                     )
-                got = jnp.sum(jnp.where(column == low, picked, 0.0), axis=0, keepdims=True)
-                to = (step * 2 + which) * blocks + block
-                values[to : to + 1, :] = got[:, 0:SLOTS]
-                values[to + 1 : to + 2, :] = got[:, SLOTS:]
+                read.append(jnp.sum(jnp.where(column == low, picked, 0.0), axis=0, keepdims=True))
+            got = read[1] - read[0]
+            to = step * blocks + block
+            values[to : to + 1, :] = got[:, 0:SLOTS]
+            values[to + 1 : to + 2, :] = got[:, SLOTS:]
     lists = values[...].astype(BF16)
     for j in range(SLABS):
         value_ref[j] = lists
 
 
-def change_kernel(value_ref, slot_ref, field_in_ref, change_out, field_out, change_ref, sems):
-    field_copy = pltpu.make_async_copy(field_in_ref, field_out, sems.at[0])
-    field_copy.start()
+def change_kernel(value_ref, slot_ref, spare_ref, change_ref):
     lines = slot_ref.shape[1]
     blocks = lines * 128 // BLOCK
+    other = spare_ref[STEPS * lines : STEPS * lines + 8, :] > 0.0
     for step in range(STEPS):
         for block in range(blocks):
-            back = []
+            change = jnp.zeros((8, 128), F32)
+            at = step * blocks + block
             for which in range(2):
                 slot = slot_ref[which * STEPS + step, block * 8 : block * 8 + 8, :]
                 rank = slot & (SLOTS - 1)
                 home = slot >> 7
-                at = (step * 2 + which) * blocks + block
                 total = jnp.zeros((8, 128), F32)
                 for j in range(SLABS):
                     line = jnp.broadcast_to(value_ref[j, at : at + 1, :].astype(F32), (8, 128))
                     total = jnp.where(home == j, jnp.take_along_axis(line, rank, axis=1), total)
-                back.append(total)
-            change = back[1] - back[0]
+                change = change + total
+            row = step * lines + block * 8
+            change = jnp.where(other, spare_ref[row : row + 8, :], change)
             for i in range(8):
                 lanes = slice((block * 8 + i) * 128, (block * 8 + i + 1) * 128)
                 change_ref[step : step + 1, lanes] = change[i : i + 1, :]
-    change_copy = pltpu.make_async_copy(change_ref, change_out, sems.at[1])
-    change_copy.start()
-    field_copy.wait()
-    change_copy.wait()
 
 
 VMEM = pl.BlockSpec(memory_space=pltpu.VMEM)
 SMEM = pl.BlockSpec(memory_space=pltpu.SMEM)
-HBM = pl.BlockSpec(memory_space=pltpu.HBM)
 ROOM = pltpu.CompilerParams(vmem_limit_bytes=24 * 2**20)
 
 
@@ -496,7 +502,7 @@
     own, slot, table = pl.pallas_call(
         functools.partial(rank_kernel, scale),
         out_shape=(
-            shape((SETS * blocks * 8, SLOTS), F32),
+            shape((STEPS * blocks * 8 + 8, SLOTS), F32),
             shape((SETS, beads // 128, 128), jnp.int32),
             shape((NX, NX), BF16),
         ),
@@ -506,8 +512,8 @@
         scratch_shapes=[
             pltpu.VMEM((SETS, beads), F32),
             pltpu.VMEM((3 * SETS, beads), F32),
-            pltpu.VMEM((SETS * chunks * 16, CHUNK), BF16),
-            pltpu.VMEM((SETS * chunks * 16, CHUNK + 128), F32),
+            pltpu.VMEM((STEPS * chunks * 16, CHUNK), BF16),
+            pltpu.VMEM((STEPS * chunks * 16, CHUNK + 128), F32),
         ],
         name="ranks",
     )(slab, code)
@@ -515,7 +521,7 @@
         field_kernel,
         out_shape=(
             shape((4, ZDEV, 2 * NX), BF16),
-            shape((SLABS, SETS * blocks, SLOTS), BF16),
+            shape((SLABS, STEPS * blocks, SLOTS), BF16),
             shape((1,), jnp.int32),
         ),
         in_specs=[SMEM] + [VMEM] * 3,
@@ -528,27 +534,31 @@
             pltpu.VMEM((STEPS * ROWS * 2, NX), BF16),
             pltpu.VMEM((STEPS, NX, ROWS * 2), F32),
             pltpu.VMEM((STEPS, NX, ROWS * 2), BF16),
-            pltpu.VMEM((SETS * blocks, SLOTS), F32),
+            pltpu.VMEM((STEPS * blocks, SLOTS), F32),
         ],
         name="fields",
     )(place, msg, own, table)
     value = lax.all_to_all(value, "grid", split_axis=0, concat_axis=0, tiled=True)
 
-    def bucketed(value, slot, field, *_):
-        return pl.pallas_call(
-            change_kernel,
-            out_shape=(shape((STEPS, beads), F32), shape(field.shape, BF16)),
-            in_specs=[VMEM] * 3,
-            out_specs=(HBM, HBM),
-            scratch_shapes=[pltpu.VMEM((STEPS, beads), F32), pltpu.SemaphoreType.DMA((2,))],
-            compiler_params=ROOM,
-            name="changes",
-        )(value, slot, field)
-
-    def general(value, slot, field, *arguments):
-        return any_spread(*arguments)
-
-    return lax.cond(crowd[0] == 1, general, bucketed, value, slot, field, cells_start, moves, accepted, bead_types)
+
+    def general(spare, field, *arguments):
+        change, field = any_spread(*arguments)
+        return jnp.concatenate([change.reshape(-1, SLOTS), jnp.ones((8, SLOTS), F32)], axis=0), field
+
+    value, own = lax.optimization_barrier((value, own))
+    spare, field = lax.cond(
+        crowd[0] == 1, general, lambda spare, field, *_: (spare, field),
+        own, field, cells_start, moves, accepted, bead_types,
+    )
+    change = pl.pallas_call(
+        change_kernel,
+        out_shape=shape((STEPS, beads), F32),
+        in_specs=[VMEM] * 3,
+        out_specs=VMEM,
+        compiler_params=ROOM,
+        name="changes",
+    )(value, slot, spare)
+    return change, field
 
 
 def solution(mesh):

time: 45.3 us -> 45 us (level)
  local copies, waits for them, and re-layouts: 0.64 us -> 0.01 us
  Pallas kernels: 14.1 us -> 13.5 us
  waiting for transfers between devices: 12.4 us -> 12.9 us
    all_to_all x1, waiting for transfers between devices: 3.47 us -> 4.58 us  [local(): msg = lax.all_to_all(msg, 'mol', split_axis=0, concat_axis=0, tiled=True)]
    pallas_call x1, Pallas kernels: 3.19 us -> 2.08 us  [local(): pl.pallas_call(functools.partial(rank_kernel, scale), out_shape=(shape((S...]
    unnamed x10 -> x6, local copies, waits for them, and re-layouts: 0.64 us -> 0.01 us
    all_to_all x1, waiting for transfers between devices: 8.94 us -> 8.33 us  [local(): lax.all_to_all(value, 'grid', split_axis=0, concat_axis=0, tiled=True)]
    pallas_call x1, Pallas kernels: 0.81 us -> 1.35 us  [local(): pl.pallas_call(change_kernel, out_shape=shape((STEPS, beads), F32), in_sp...]
  transfers between devices with their start and end apart: 2 -> 2, of which waited for: 2 -> 2; matrix products, arithmetic and copies ran while one was open for 0% -> 0% of each run, Pallas kernels for 7% -> 5%
where the time goes in v4:
time: 45 us; the launch traced here: 44.3 us
  starting transfers between devices  16.3 us (36%)
  Pallas kernels  13.5 us (30%)
  waiting for transfers between devices  12.9 us (29%)
  between operations  1.39 us (3%)
    all_to_all x1, starting transfers between devices, local(): lax.all_to_all(value, 'grid', split_axis=0, concat_axis=0, tiled=True)  10.8 us
    all_to_all x1, waiting for transfers between devices, local(): lax.all_to_all(value, 'grid', split_axis=0, concat_axis=0, tiled=True)  8.33 us
    pallas_call x1, Pallas kernels, local(): pl.pallas_call(field_kernel, out_shape=(shape((4, ZDEV, 2 * NX), BF16), s...  6.47 us
    all_to_all x1, starting transfers between devices, local(): msg = lax.all_to_all(msg, 'mol', split_axis=0, concat_axis=0, tiled=True)  5.5 us
    all_to_all x1, waiting for transfers between devices, local(): msg = lax.all_to_all(msg, 'mol', split_axis=0, concat_axis=0, tiled=True)  4.58 us
    pallas_call x1, Pallas kernels, local(): pl.pallas_call(bucket_kernel, out_shape=(shape((SLABS, 32, SLOTS), BF16),...  3.64 us
    pallas_call x1, Pallas kernels, local(): pl.pallas_call(functools.partial(rank_kernel, scale), out_shape=(shape((S...  2.08 us
    pallas_call x1, Pallas kernels, local(): pl.pallas_call(change_kernel, out_shape=shape((STEPS, beads), F32), in_sp...  1.35 us
  transfers between devices with their start and end apart: 2, of which 2 were waited for; matrix products, arithmetic and copies ran while one was open for 0% of the time, Pallas kernels for 5%

profile of v4, /device:TPU:32, one launch (start us, length us, event | category | flops | bytes accessed | tf_op | source)
XLA Modules:
  0.0 44.3 jit_solution(17905404155069066182)
XLA Ops:
  0.6 0.0 copy-start.1
  0.6 0.0 copy-start
  0.6 0.0 copy-start.4
  0.7 3.6 %bucket.1 = (bf16[16,32,128]{2,1,0:T(8,128)(2,1)}, s32[4,8192]{1,0:T(4,128)S(1)}) custom-call(s32[1]{0:T(128)} %bitcast.11.slab_ref, s32[1,8192]{1,0:T(1,128)} %bitcast.31, s32[3,2,8192]{2,1,0:T(2,128)} %bitcast.28, s32[2,8192]{1,0:T(2,128)} %accepted_ref.1, s32[1,8192]{1,0:T(1,128)} %bitcast.14.types_ref), custom_call_target="tpu_custom_call" | custom-call | tf_op jit(solution)/shard_map/bucket/pallas_call | solution.py:485
  4.3 5.5 %all-to-all-start.6 = ((bf16[16,32,128]{2,1,0:T(8,128)(2,1)}), bf16[16,32,128]{2,1,0:T(8,128)(2,1)S(1)}, u32[]{:S(2)}, u32[]{:S(2)}) async-start(bf16[16,32,128]{2,1,0:T(8,128)(2,1)} %get-tuple-element.249), calls=%async_computation.6 | async-start | bytes 262144 | tf_op jit(solution)/shard_map/all_to_all | solution.py:501
  9.8 2.1 %ranks.1 = (f32[136,128]{1,0:T(8,128)S(1)}, s32[4,64,128]{2,1,0:T(8,128)S(1)}, bf16[512,512]{1,0:T(8,128)(2,1)S(1)}) custom-call(s32[1]{0:T(128)} %bitcast.11.slab_ref, s32[4,8192]{1,0:T(4,128)S(1)} %get-tuple-element.250.code_ref), custom_call_target="tpu_custom_call" | custom-call | tf_op jit(solution)/shard_map/ranks/pallas_call | solution.py:502
  11.9 4.6 %all-to-all-done.6.msg_ref = bf16[16,32,128]{2,1,0:T(8,128)(2,1)S(1)} async-done(((bf16[16,32,128]{2,1,0:T(8,128)(2,1)}), bf16[16,32,128]{2,1,0:T(8,128)(2,1)S(1)}, u32[]{:S(2)}, u32[]{:S(2)}) %all-to-all-start.6) | async-done | bytes 131104 | tf_op jit(solution)/shard_map/all_to_all | solution.py:501
  16.5 6.5 %fields.1 = (bf16[4,4,1024]{2,1,0:T(4,128)(2,1)}, bf16[16,16,128]{2,1,0:T(8,128)(2,1)}, s32[1]{0:T(128)}) custom-call(s32[1]{0:T(128)} %bitcast.10.place_ref, bf16[16,32,128]{2,1,0:T(8,128)(2,1)S(1)} %all-to-all-done.6.msg_ref, f32[136,128]{1,0:T(8,128)S(1)} %get-tuple-element.257.own_ref, bf16[512,512]{1,0:T(8,128)(2,1)S(1)} %get-tuple-element.252.table_ref), custom_call_target="tpu_custom_call" | custom-call | tf_op jit(solution)/shard_map/fields/pallas_call | solution.py:520
  23.0 10.8 %all-to-all-start.7 = ((bf16[16,16,128]{2,1,0:T(8,128)(2,1)}), bf16[16,16,128]{2,1,0:T(8,128)(2,1)S(1)}, u32[]{:S(2)}, u32[]{:S(2)}) async-start(bf16[16,16,128]{2,1,0:T(8,128)(2,1)} %get-tuple-element.253), calls=%async_computation.7 | async-start | bytes 131072 | tf_op jit(solution)/shard_map/all_to_all | solution.py:541
  34.4 8.3 %all-to-all-done.7.value_ref = bf16[16,16,128]{2,1,0:T(8,128)(2,1)S(1)} async-done(((bf16[16,16,128]{2,1,0:T(8,128)(2,1)}), bf16[16,16,128]{2,1,0:T(8,128)(2,1)S(1)}, u32[]{:S(2)}, u32[]{:S(2)}) %all-to-all-start.7) | async-done | bytes 65568 | tf_op jit(solution)/shard_map/all_to_all | solution.py:541
  42.7 0.0 copy-done.1
  42.7 0.0 copy-done
  42.7 0.0 copy-done.4
  42.7 0.2 conditional.1
  43.0 1.3 %changes.1 = f32[2,8192]{1,0:T(2,128)} custom-call(bf16[16,16,128]{2,1,0:T(8,128)(2,1)S(1)} %all-to-all-done.7.value_ref, s32[4,64,128]{2,1,0:T(8,128)S(1)} %get-tuple-element.255.slot_ref, f32[136,128]{1,0:T(8,128)S(1)} %get-tuple-element.259.spare_ref), custom_call_target="tpu_custom_call" | custom-call | tf_op jit(solution)/shard_map/changes/pallas_call | solution.py:553
Async XLA Ops:
  0.6 42.1 %copy-start.1 = (s32[8192]{0:T(1024)S(1)}, s32[8192]{0:T(1024)}, u32[]{:S(2)}) copy-start(s32[8192]{0:T(1024)} %param.12) | copy-start | bytes 98308
  0.6 42.1 %copy-start = (s32[2,3,8192]{2,0,1:T(2,128)S(1)}, s32[2,3,8192]{2,0,1:T(2,128)}, u32[]{:S(2)}) copy-start(s32[2,3,8192]{2,0,1:T(2,128)} %param.13) | copy-start | bytes 589828
  0.6 42.1 %copy-start.4 = (s32[2,8192]{1,0:T(2,128)S(1)}, s32[2,8192]{1,0:T(2,128)}, u32[]{:S(2)}) copy-start(s32[2,8192]{1,0:T(2,128)} %accepted_ref.1) | copy-start | bytes 196612
  4.3 12.2 %all-to-all-start.6 = ((bf16[16,32,128]{2,1,0:T(8,128)(2,1)}), bf16[16,32,128]{2,1,0:T(8,128)(2,1)S(1)}, u32[]{:S(2)}, u32[]{:S(2)}) async-start(bf16[16,32,128]{2,1,0:T(8,128)(2,1)} %get-tuple-element.249), calls=%async_computation.6 | async-start | bytes 262144 | tf_op jit(solution)/shard_map/all_to_all | solution.py:501
  23.0 19.8 %all-to-all-start.7 = ((bf16[16,16,128]{2,1,0:T(8,128)(2,1)}), bf16[16,16,128]{2,1,0:T(8,128)(2,1)S(1)}, u32[]{:S(2)}, u32[]{:S(2)}) async-start(bf16[16,16,128]{2,1,0:T(8,128)(2,1)} %get-tuple-element.253), calls=%async_computation.7 | async-start | bytes 131072 | tf_op jit(solution)/shard_map/all_to_all | solution.py:541

commit v5 on v4

--- a/solution.py
+++ b/solution.py
@@ -432,8 +432,8 @@
                         one_hot(jnp.where(part == q + 1.0, row, -1.0), ROWS),
                         preferred_element_type=F32,
                     )
-                read.append(jnp.sum(jnp.where(column == low, picked, 0.0), axis=0, keepdims=True))
-            got = read[1] - read[0]
+                read.append(jnp.where(column == low, picked, 0.0))
+            got = jnp.sum(read[1] - read[0], axis=0, keepdims=True)
             to = step * blocks + block
             values[to : to + 1, :] = got[:, 0:SLOTS]
             values[to + 1 : to + 2, :] = got[:, SLOTS:]

time: 45 us -> 45 us (level)
  no operation moved by 1% of the time
where the time goes in v5:
time: 45 us; the launch traced here: 44.3 us
  starting transfers between devices  16.3 us (36%)
  Pallas kernels  13.5 us (30%)
  waiting for transfers between devices  12.9 us (29%)
  between operations  1.39 us (3%)
    all_to_all x1, starting transfers between devices, local(): lax.all_to_all(value, 'grid', split_axis=0, concat_axis=0, tiled=True)  10.8 us
    all_to_all x1, waiting for transfers between devices, local(): lax.all_to_all(value, 'grid', split_axis=0, concat_axis=0, tiled=True)  8.33 us
    pallas_call x1, Pallas kernels, local(): pl.pallas_call(field_kernel, out_shape=(shape((4, ZDEV, 2 * NX), BF16), s...  6.47 us
    all_to_all x1, starting transfers between devices, local(): msg = lax.all_to_all(msg, 'mol', split_axis=0, concat_axis=0, tiled=True)  5.5 us
    all_to_all x1, waiting for transfers between devices, local(): msg = lax.all_to_all(msg, 'mol', split_axis=0, concat_axis=0, tiled=True)  4.58 us
    pallas_call x1, Pallas kernels, local(): pl.pallas_call(bucket_kernel, out_shape=(shape((SLABS, 32, SLOTS), BF16),...  3.64 us
    pallas_call x1, Pallas kernels, local(): pl.pallas_call(functools.partial(rank_kernel, scale), out_shape=(shape((S...  2.08 us
    pallas_call x1, Pallas kernels, local(): pl.pallas_call(change_kernel, out_shape=shape((STEPS, beads), F32), in_sp...  1.35 us
  transfers between devices with their start and end apart: 2, of which 2 were waited for; matrix products, arithmetic and copies ran while one was open for 0% of the time, Pallas kernels for 5%

profile of v5, /device:TPU:32, one launch (start us, length us, event | category | flops | bytes accessed | tf_op | source)
XLA Modules:
  0.0 44.3 jit_solution(17292391286354175427)
XLA Ops:
  0.6 0.0 copy-start.1
  0.6 0.0 copy-start
  0.6 0.0 copy-start.4
  0.7 3.6 %bucket.1 = (bf16[16,32,128]{2,1,0:T(8,128)(2,1)}, s32[4,8192]{1,0:T(4,128)S(1)}) custom-call(s32[1]{0:T(128)} %bitcast.11.slab_ref, s32[1,8192]{1,0:T(1,128)} %bitcast.31, s32[3,2,8192]{2,1,0:T(2,128)} %bitcast.28, s32[2,8192]{1,0:T(2,128)} %accepted_ref.1, s32[1,8192]{1,0:T(1,128)} %bitcast.14.types_ref), custom_call_target="tpu_custom_call" | custom-call | tf_op jit(solution)/shard_map/bucket/pallas_call | solution.py:485
  4.3 5.5 %all-to-all-start.6 = ((bf16[16,32,128]{2,1,0:T(8,128)(2,1)}), bf16[16,32,128]{2,1,0:T(8,128)(2,1)S(1)}, u32[]{:S(2)}, u32[]{:S(2)}) async-start(bf16[16,32,128]{2,1,0:T(8,128)(2,1)} %get-tuple-element.249), calls=%async_computation.6 | async-start | bytes 262144 | tf_op jit(solution)/shard_map/all_to_all | solution.py:501
  9.8 2.1 %ranks.1 = (f32[136,128]{1,0:T(8,128)S(1)}, s32[4,64,128]{2,1,0:T(8,128)S(1)}, bf16[512,512]{1,0:T(8,128)(2,1)S(1)}) custom-call(s32[1]{0:T(128)} %bitcast.11.slab_ref, s32[4,8192]{1,0:T(4,128)S(1)} %get-tuple-element.250.code_ref), custom_call_target="tpu_custom_call" | custom-call | tf_op jit(solution)/shard_map/ranks/pallas_call | solution.py:502
  11.9 4.6 %all-to-all-done.6.msg_ref = bf16[16,32,128]{2,1,0:T(8,128)(2,1)S(1)} async-done(((bf16[16,32,128]{2,1,0:T(8,128)(2,1)}), bf16[16,32,128]{2,1,0:T(8,128)(2,1)S(1)}, u32[]{:S(2)}, u32[]{:S(2)}) %all-to-all-start.6) | async-done | bytes 131104 | tf_op jit(solution)/shard_map/all_to_all | solution.py:501
  16.5 6.5 %fields.1 = (bf16[4,4,1024]{2,1,0:T(4,128)(2,1)}, bf16[16,16,128]{2,1,0:T(8,128)(2,1)}, s32[1]{0:T(128)}) custom-call(s32[1]{0:T(128)} %bitcast.10.place_ref, bf16[16,32,128]{2,1,0:T(8,128)(2,1)S(1)} %all-to-all-done.6.msg_ref, f32[136,128]{1,0:T(8,128)S(1)} %get-tuple-element.257.own_ref, bf16[512,512]{1,0:T(8,128)(2,1)S(1)} %get-tuple-element.252.table_ref), custom_call_target="tpu_custom_call" | custom-call | tf_op jit(solution)/shard_map/fields/pallas_call | solution.py:520
  23.0 10.8 %all-to-all-start.7 = ((bf16[16,16,128]{2,1,0:T(8,128)(2,1)}), bf16[16,16,128]{2,1,0:T(8,128)(2,1)S(1)}, u32[]{:S(2)}, u32[]{:S(2)}) async-start(bf16[16,16,128]{2,1,0:T(8,128)(2,1)} %get-tuple-element.253), calls=%async_computation.7 | async-start | bytes 131072 | tf_op jit(solution)/shard_map/all_to_all | solution.py:541
  34.4 8.3 %all-to-all-done.7.value_ref = bf16[16,16,128]{2,1,0:T(8,128)(2,1)S(1)} async-done(((bf16[16,16,128]{2,1,0:T(8,128)(2,1)}), bf16[16,16,128]{2,1,0:T(8,128)(2,1)S(1)}, u32[]{:S(2)}, u32[]{:S(2)}) %all-to-all-start.7) | async-done | bytes 65568 | tf_op jit(solution)/shard_map/all_to_all | solution.py:541
  42.7 0.0 copy-done.1
  42.7 0.0 copy-done
  42.7 0.0 copy-done.4
  42.7 0.2 conditional.1
  43.0 1.3 %changes.1 = f32[2,8192]{1,0:T(2,128)} custom-call(bf16[16,16,128]{2,1,0:T(8,128)(2,1)S(1)} %all-to-all-done.7.value_ref, s32[4,64,128]{2,1,0:T(8,128)S(1)} %get-tuple-element.255.slot_ref, f32[136,128]{1,0:T(8,128)S(1)} %get-tuple-element.259.spare_ref), custom_call_target="tpu_custom_call" | custom-call | tf_op jit(solution)/shard_map/changes/pallas_call | solution.py:553
Async XLA Ops:
  0.6 42.1 %copy-start.1 = (s32[8192]{0:T(1024)S(1)}, s32[8192]{0:T(1024)}, u32[]{:S(2)}) copy-start(s32[8192]{0:T(1024)} %param.12) | copy-start | bytes 98308
  0.6 42.1 %copy-start = (s32[2,3,8192]{2,0,1:T(2,128)S(1)}, s32[2,3,8192]{2,0,1:T(2,128)}, u32[]{:S(2)}) copy-start(s32[2,3,8192]{2,0,1:T(2,128)} %param.13) | copy-start | bytes 589828
  0.6 42.1 %copy-start.4 = (s32[2,8192]{1,0:T(2,128)S(1)}, s32[2,8192]{1,0:T(2,128)}, u32[]{:S(2)}) copy-start(s32[2,8192]{1,0:T(2,128)} %accepted_ref.1) | copy-start | bytes 196612
  4.3 12.2 %all-to-all-start.6 = ((bf16[16,32,128]{2,1,0:T(8,128)(2,1)}), bf16[16,32,128]{2,1,0:T(8,128)(2,1)S(1)}, u32[]{:S(2)}, u32[]{:S(2)}) async-start(bf16[16,32,128]{2,1,0:T(8,128)(2,1)} %get-tuple-element.249), calls=%async_computation.6 | async-start | bytes 262144 | tf_op jit(solution)/shard_map/all_to_all | solution.py:501
  23.0 19.8 %all-to-all-start.7 = ((bf16[16,16,128]{2,1,0:T(8,128)(2,1)}), bf16[16,16,128]{2,1,0:T(8,128)(2,1)S(1)}, u32[]{:S(2)}, u32[]{:S(2)}) async-start(bf16[16,16,128]{2,1,0:T(8,128)(2,1)} %get-tuple-element.253), calls=%async_computation.7 | async-start | bytes 131072 | tf_op jit(solution)/shard_map/all_to_all | solution.py:541
